TPU v7x, 32 devices: a whole 2x2x4 slice. The times are simulated.
32 devices in a mesh: lat: 16 (over z, x, core), lon: 2 (over y).
Axes of the slice: x: 2, y: 2, z: 4, core: 2. Of those that a mesh axis runs over, the one named last changes fastest.
Arguments:
- elevation: float32 [4096, 4096], P('lat', 'lon'), may hold values from -200 to 200
Outputs:
- slope_angle: float32 [4096, 4096], P('lat', 'lon')
- facing: float32 [2, 4096, 4096], P(None, 'lat', 'lon')
- hillshade: float32 [4096, 4096], P('lat', 'lon')
All inputs are finite; a program needn't handle non-finite values.
Results may differ from a plain program's by a relative error of at most 0.0003.
Values sent between devices are 32-bit elements; how exact they have to be, the bound alone decides.
No kernel may reach another device: no remote copies, remote signals or barrier semaphores. Data moves between devices by JAX's collectives and lax.ppermute only.
A program may use at most 64 MiB of HBM per device.

v0:
```python
import math

import jax
import jax.numpy as jnp
from jax import lax
from jax.sharding import PartitionSpec as P

SCALES = 7
HALO = 64


LIGHT_EAST = -0.5
LIGHT_NORTH = 0.5
LIGHT_UP = math.sqrt(0.5)


def padded_2(block, sides, width, periodic):
    for axis, dim in sides:
        count = lax.axis_size(axis)
        forward = [(i, i + 1) for i in range(count - 1)]
        if periodic:
            forward.append((count - 1, 0))
        backward = [(target, source) for source, target in forward]
        low = lax.ppermute(
            lax.slice_in_dim(block, block.shape[dim] - width, None, axis=dim), axis, forward
        )
        high = lax.ppermute(lax.slice_in_dim(block, 0, width, axis=dim), axis, backward)
        block = jnp.concatenate([low, block, high], axis=dim)
    return block


def window(padded, margin, row_offset, col_offset, row_count, col_count):
    return lax.slice(
        padded,
        (margin + row_offset, margin + col_offset),
        (margin + row_offset + row_count, margin + col_offset + col_count),
    )


def terrain_shading(padded, spacing, margin, levels):
    row_count = padded.shape[0] - 2 * margin
    col_count = padded.shape[1] - 2 * margin
    eastward = jnp.zeros((row_count, col_count), jnp.float32)
    northward = jnp.zeros((row_count, col_count), jnp.float32)
    for octave in range(levels):
        stride = 2**octave
        north_west = window(padded, margin, -stride, -stride, row_count, col_count)
        north_mid = window(padded, margin, -stride, 0, row_count, col_count)
        north_east = window(padded, margin, -stride, stride, row_count, col_count)
        west_mid = window(padded, margin, 0, -stride, row_count, col_count)
        east_mid = window(padded, margin, 0, stride, row_count, col_count)
        south_west = window(padded, margin, stride, -stride, row_count, col_count)
        south_mid = window(padded, margin, stride, 0, row_count, col_count)
        south_east = window(padded, margin, stride, stride, row_count, col_count)
        east_diff = (
            north_east + 2.0 * east_mid + south_east - (north_west + 2.0 * west_mid + south_west)
        )
        north_diff = (
            north_west + 2.0 * north_mid + north_east - (south_west + 2.0 * south_mid + south_east)
        )
        eastward = eastward + east_diff * (1.0 / stride)
        northward = northward + north_diff * (1.0 / stride)
    grad_east = eastward / (8.0 * levels * spacing[:, None])
    grad_north = northward * (1.0 / (8.0 * levels))
    squared = grad_east * grad_east + grad_north * grad_north
    slope_angle = jnp.arctan(jnp.sqrt(squared))
    inverse = lax.rsqrt(1.0 + squared)
    facing_east = -grad_east * inverse
    facing_north = -grad_north * inverse
    shading = jnp.maximum(
        LIGHT_EAST * facing_east + LIGHT_NORTH * facing_north + LIGHT_UP * inverse, 0.0
    )
    return (slope_angle, jnp.stack([facing_east, facing_north]), shading)


def pole_clamp(padded, margin):
    lat_index = lax.axis_index("lat")
    last_index = lax.axis_size("lat") - 1
    padded_rows = padded.shape[0]
    position = lax.broadcasted_iota(jnp.int32, (padded_rows, 1), 0)
    top_row = padded[margin : margin + 1]
    bottom_row = padded[padded_rows - margin - 1 : padded_rows - margin]
    above = jnp.logical_and(position < margin, lat_index == 0)
    below = jnp.logical_and(position >= padded_rows - margin, lat_index == last_index)
    return jnp.where(above, top_row, jnp.where(below, bottom_row, padded))


def with_rims(elevation, margin):
    broad_tile = padded_2(elevation, (("lon", 1),), margin, True)
    broad_tile = padded_2(broad_tile, (("lat", 0),), margin, False)
    return pole_clamp(broad_tile, margin)


def local(elevation):
    row_count, col_count = elevation.shape
    total_rows = row_count * lax.axis_size("lat")
    total_cols = col_count * lax.axis_size("lon")
    margin = HALO
    position = lax.axis_index("lat") * row_count + lax.iota(jnp.int32, row_count)
    spacing = jnp.sin((position.astype(jnp.float32) + 0.5) * (math.pi / total_rows)) * (
        2.0 * total_rows / total_cols
    )
    padded = with_rims(elevation, margin)
    return terrain_shading(padded, spacing, margin, SCALES)


def solution(mesh):
    in_specs = (P("lat", "lon"),)
    out_specs = (P("lat", "lon"), P(None, "lat", "lon"), P("lat", "lon"))
    return jax.shard_map(local, mesh=mesh, in_specs=in_specs, out_specs=out_specs, check_vma=False)
```

profile of v0, /device:TPU:9, one launch (start us, length us, event | category | flops | bytes accessed | tf_op | source)
XLA Modules:
  0.0 68.1 jit_solution(1316667555564179711)
XLA Ops:
  0.6 1.1 %fusion.104 = (f32[256,64]{1,0:T(8,128)S(1)}, f32[256,64]{1,0:T(8,128)S(1)}) fusion(f32[256,2048]{1,0:T(8,128)} %param.1), kind=kLoop, calls=%fused_computation.143 | loop fusion | bytes 262144 | tf_op jit(solution)/shard_map/slice | solution.py:27
  1.7 1.3 %collective-permute-start.1 = (f32[256,64]{1,0:T(8,128)S(1)}, f32[256,64]{1,0:T(8,128)S(1)}, u32[]{:S(2)}, u32[]{:S(2)}) collective-permute-start(f32[256,64]{1,0:T(8,128)S(1)} %get-tuple-element.13), channel_id=1, source_target_pairs={{1,0},{0,1},{3,2},{2,3},{5,4},{4,5},{7,6},{6,7},{9,8},{8,9},{11,10... | collective-permute-start | bytes 196616 | tf_op jit(solution)/shard_map/ppermute | solution.py:27
  3.0 0.2 collective-permute-start
  3.2 2.9 %collective-permute-done.1 = f32[256,64]{1,0:T(8,128)S(1)} collective-permute-done((f32[256,64]{1,0:T(8,128)S(1)}, f32[256,64]{1,0:T(8,128)S(1)}, u32[]{:S(2)}, u32[]{:S(2)}) %collective-permute-start.1) | collective-permute-done | bytes 65568 | tf_op jit(solution)/shard_map/ppermute | solution.py:27
  6.1 2.8 %collective-permute-done = f32[256,64]{1,0:T(8,128)S(1)} collective-permute-done((f32[256,64]{1,0:T(8,128)S(1)}, f32[256,64]{1,0:T(8,128)S(1)}, u32[]{:S(2)}, u32[]{:S(2)}) %collective-permute-start) | collective-permute-done | bytes 65568 | tf_op jit(solution)/shard_map/ppermute | solution.py:24
  9.0 3.0 %concatenate.6 = f32[256,2176]{1,0:T(8,128)S(1)} concatenate(f32[256,64]{1,0:T(8,128)S(1)} %collective-permute-done, f32[256,2048]{1,0:T(8,128)} %param.1, f32[256,64]{1,0:T(8,128)S(1)} %collective-permute-done.1), dimensions={1} | concatenate | bytes 4456448 | tf_op jit(solution)/shard_map/concatenate | solution.py:28
  11.9 0.1 fusion.103
  12.0 4.5 %collective-permute-start.2 = (f32[64,2176]{1,0:T(8,128)S(1)}, f32[64,2176]{1,0:T(8,128)}, u32[]{:S(2)}, u32[]{:S(2)}) collective-permute-start(f32[64,2176]{1,0:T(8,128)S(1)} %get-tuple-element.11), channel_id=1, source_target_pairs={{0,2},{2,4},{4,6},{6,8},{8,10},{10,12},{12,14},{14,16},{16,18},{18... | collective-permute-start | bytes 1671176 | tf_op jit(solution)/shard_map/ppermute | solution.py:24
  16.6 1.9 %collective-permute-start.3 = (f32[64,2176]{1,0:T(8,128)S(1)}, f32[64,2176]{1,0:T(8,128)}, u32[]{:S(2)}, u32[]{:S(2)}) collective-permute-start(f32[64,2176]{1,0:T(8,128)S(1)} %get-tuple-element.12), channel_id=1, source_target_pairs={{2,0},{4,2},{6,4},{8,6},{10,8},{12,10},{14,12},{16,14},{18,16},{20... | collective-permute-start | bytes 1671176 | tf_op jit(solution)/shard_map/ppermute | solution.py:27
  18.6 10.4 %collective-permute-done.2 = f32[64,2176]{1,0:T(8,128)} collective-permute-done((f32[64,2176]{1,0:T(8,128)S(1)}, f32[64,2176]{1,0:T(8,128)}, u32[]{:S(2)}, u32[]{:S(2)}) %collective-permute-start.2) | collective-permute-done | bytes 557088 | tf_op jit(solution)/shard_map/ppermute | solution.py:24
  29.0 1.7 %collective-permute-done.3 = f32[64,2176]{1,0:T(8,128)} collective-permute-done((f32[64,2176]{1,0:T(8,128)S(1)}, f32[64,2176]{1,0:T(8,128)}, u32[]{:S(2)}, u32[]{:S(2)}) %collective-permute-start.3) | collective-permute-done | bytes 557088 | tf_op jit(solution)/shard_map/ppermute | solution.py:27
  30.7 1.7 %fusion = f32[384,2176]{1,0:T(8,128)S(1)} fusion(f32[64,2176]{1,0:T(8,128)} %collective-permute-done.3, f32[256,2176]{1,0:T(8,128)S(1)} %concatenate.6, f32[64,2176]{1,0:T(8,128)} %collective-permute-done.2, f32[2176]{0:T(1024)S(1)} %get-tuple-element.4, f32[2176]{0:T(1024)S(1)} %get-tuple-element.3, pred[384]{0:T(512)(128)(4,1)S(1)} %get-tuple-element.16, ...), kind=kLoop, calls=%fused_computation.2 | loop fusion | flops 3342336 | bytes 6702848 | tf_op jit(solution)/shard_map/jit(_where)/select_n | solution.py:85
  32.3 28.6 %add_maximum_fusion = (f32[256,2048]{1,0:T(8,128)}, f32[256,2048]{1,0:T(8,128)S(1)}, f32[256,2048]{1,0:T(8,128)S(1)}) fusion(f32[256]{0:T(256)S(1)} %sine_multiply_fusion, f32[384,2176]{1,0:T(8,128)S(1)} %fusion), kind=kLoop, calls=%fused_computation.127 | loop fusion | flops 72351744 | bytes 123732992 | tf_op jit(solution)/shard_map/max | solution.py:70
  60.9 4.6 %fusion.97 = (f32[1,256,2048]{2,1,0:T(8,128)S(1)}, f32[1,256,2048]{2,1,0:T(8,128)S(1)}, f32[256,2048]{1,0:T(8,128)}) fusion(f32[256,2048]{1,0:T(8,128)S(1)} %get-tuple-element.6, f32[256,2048]{1,0:T(8,128)S(1)} %get-tuple-element.7), kind=kLoop, calls=%fused_computation.133 | loop fusion | flops 4194304 | bytes 10485760 | tf_op jit(solution)/shard_map/stack | solution.py:73
  65.5 2.5 %pad_maximum_fusion = f32[2,256,2048]{2,1,0:T(8,128)} fusion(f32[1,256,2048]{2,1,0:T(8,128)S(1)} %get-tuple-element.9, f32[1,256,2048]{2,1,0:T(8,128)S(1)} %get-tuple-element.8), kind=kLoop, calls=%fused_computation | loop fusion | flops 1048576 | bytes 8388608 | tf_op jit(solution)/shard_map/stack | solution.py:73
  (3 shorter events, 0.1 us)
Async XLA Ops:
  1.7 4.4 %collective-permute-start.1 = (f32[256,64]{1,0:T(8,128)S(1)}, f32[256,64]{1,0:T(8,128)S(1)}, u32[]{:S(2)}, u32[]{:S(2)}) collective-permute-start(f32[256,64]{1,0:T(8,128)S(1)} %get-tuple-element.13), channel_id=1, source_target_pairs={{1,0},{0,1},{3,2},{2,3},{5,4},{4,5},{7,6},{6,7},{9,8},{8,9},{11,10... | collective-permute-start | bytes 196616 | tf_op jit(solution)/shard_map/ppermute | solution.py:27
  3.0 6.0 %collective-permute-start = (f32[256,64]{1,0:T(8,128)S(1)}, f32[256,64]{1,0:T(8,128)S(1)}, u32[]{:S(2)}, u32[]{:S(2)}) collective-permute-start(f32[256,64]{1,0:T(8,128)S(1)} %get-tuple-element.14), channel_id=1, source_target_pairs={{0,1},{1,0},{2,3},{3,2},{4,5},{5,4},{6,7},{7,6},{8,9},{9,8},{10,11... | collective-permute-start | bytes 196616 | tf_op jit(solution)/shard_map/ppermute | solution.py:24
  12.0 17.0 %collective-permute-start.2 = (f32[64,2176]{1,0:T(8,128)S(1)}, f32[64,2176]{1,0:T(8,128)}, u32[]{:S(2)}, u32[]{:S(2)}) collective-permute-start(f32[64,2176]{1,0:T(8,128)S(1)} %get-tuple-element.11), channel_id=1, source_target_pairs={{0,2},{2,4},{4,6},{6,8},{8,10},{10,12},{12,14},{14,16},{16,18},{18... | collective-permute-start | bytes 1671176 | tf_op jit(solution)/shard_map/ppermute | solution.py:24
  16.6 14.1 %collective-permute-start.3 = (f32[64,2176]{1,0:T(8,128)S(1)}, f32[64,2176]{1,0:T(8,128)}, u32[]{:S(2)}, u32[]{:S(2)}) collective-permute-start(f32[64,2176]{1,0:T(8,128)S(1)} %get-tuple-element.12), channel_id=1, source_target_pairs={{2,0},{4,2},{6,4},{8,6},{10,8},{12,10},{14,12},{16,14},{18,16},{20... | collective-permute-start | bytes 1671176 | tf_op jit(solution)/shard_map/ppermute | solution.py:27
where the time goes:
time: 68.3 us; the launch traced here: 68.1 us
  other arithmetic  37.4 us (55%)
  waiting for transfers between devices  17.8 us (26%)
  starting transfers between devices  7.99 us (12%)
  local copies, waits for them, and re-layouts  4.15 us (6%)
  between operations  0.7 us (1%)
    max x1, other arithmetic, terrain_shading(): jnp.maximum(LIGHT_EAST * facing_east + LIGHT_NORTH * facing_north + LIGHT...  28.6 us
    ppermute x2, waiting for transfers between devices, padded_2(): lax.ppermute(lax.slice_in_dim(block, block.shape[dim] - width, None, axis...  13.2 us
    another operation x2, other arithmetic, terrain_shading(): return (slope_angle, jnp.stack([facing_east, facing_north]), shading)  7.15 us
    ppermute x2, starting transfers between devices, padded_2(): lax.ppermute(lax.slice_in_dim(block, block.shape[dim] - width, None, axis...  4.76 us
    ppermute x2, waiting for transfers between devices, padded_2(): lax.ppermute(lax.slice_in_dim(block, 0, width, axis=dim), axis, backward)  4.61 us
    ppermute x2, starting transfers between devices, padded_2(): lax.ppermute(lax.slice_in_dim(block, 0, width, axis=dim), axis, backward)  3.23 us
    concatenate x1, local copies, waits for them, and re-layouts, padded_2(): block = jnp.concatenate([low, block, high], axis=dim)  2.97 us
    select_n x1, other arithmetic, pole_clamp(): return jnp.where(above, top_row, jnp.where(below, bottom_row, padded))  1.66 us
  transfers between devices with their start and end apart: 4, of which 4 were waited for; matrix products, arithmetic and copies ran while one was open for 0% of the time, Pallas kernels for 0%

commit v1 on v0

v1 whole, which is shorter than its diff:
```python
import functools
import math

import jax
import jax.numpy as jnp
from jax import lax
from jax.experimental import pallas as pl
from jax.experimental.pallas import tpu as pltpu
from jax.sharding import PartitionSpec as P

SCALES = 7
HALO = 64
LANES = 128
SUB = 8

LIGHT_UP = math.sqrt(0.5)
TINY = 1.17549435e-38

ACOS_FIT = (
    0.036142768221257435,
    -0.1987486877325598,
    0.5130441168137142,
    -0.9077345836840529,
    1.5572964573334291,
)
ANGLE_FIT = tuple(
    c * math.sqrt(2.0) * math.sqrt(0.5) ** (len(ACOS_FIT) - 1 - i) for i, c in enumerate(ACOS_FIT)
)


def shade(east, north, east_scale):
    neg_east = east * east_scale
    neg_north = north * (-1.0 / (8.0 * SCALES))
    squared = neg_east * neg_east + neg_north * neg_north
    inverse = lax.rsqrt(1.0 + squared)
    facing_east = neg_east * inverse
    facing_north = neg_north * inverse
    shading = jnp.maximum(inverse * (0.5 * (neg_north - neg_east) + LIGHT_UP), 0.0)
    sine = squared * lax.rsqrt(jnp.maximum(squared, TINY)) * inverse
    cos_one = 1.0 + inverse
    root = lax.rsqrt(cos_one)
    half = cos_one * root
    fit = ANGLE_FIT[0]
    for coefficient in ANGLE_FIT[1:]:
        fit = fit * half + coefficient
    slope = sine * root * fit
    return slope, facing_east, facing_north, shading


def stencil(z, q, scale, out, row_count, tiles):
    lane = lax.broadcasted_iota(jnp.int32, (SUB, LANES), 1)
    lags = [2**k for k in range(SCALES)]

    def steps(lag):
        return -(-lag // SUB)

    def new_boxes(base, active, tile_cache):
        here = [z[j, pl.ds(base + HALO, SUB), :] for j in range(tiles + 1)]
        for k in active:
            s = lags[k]
            pairs = []
            for j in range(tiles + 1):
                pair = z[j, pl.ds(base + HALO + s, SUB), :] + here[j]
                pairs.append(pair * (1.0 / s) if k else pair)
            if 2 * s == LANES:
                halves = [
                    pltpu.roll(jnp.where(lane >= s, pairs[j], pairs[(j + 1) % (tiles + 1)]), s, 1)
                    for j in range(tiles + 1)
                ]
            for j in range(tiles):
                before, after = pairs[(j - 1) % (tiles + 1)], pairs[j + 1]
                if 2 * s == LANES:
                    west, east = halves[(j - 1) % (tiles + 1)], halves[j]
                else:
                    west = pltpu.roll(jnp.where(lane < LANES - s, pairs[j], before), s, 1)
                    east = pltpu.roll(jnp.where(lane >= s, pairs[j], after), LANES - s, 1)
                low, high = pairs[j] + west, pairs[j] + east
                old = tile_cache.get("old") is not None
                if s < SUB:
                    q[k][0, j, pl.ds(base + s + SUB, SUB), :] = low
                    q[k][1, j, pl.ds(base + s + SUB, SUB), :] = high
                    if old:
                        before = q[k][0, j, pl.ds(base + SUB, SUB), :]
                        after = q[k][1, j, pl.ds(base + SUB, SUB), :]
                else:
                    slot = lax.bitwise_and(base // SUB, s // SUB - 1)
                    row = pl.multiple_of(slot * SUB, SUB)
                    if old:
                        before = q[k][0, j, pl.ds(row, SUB), :]
                        after = q[k][1, j, pl.ds(row, SUB), :]
                    q[k][0, j, pl.ds(row, SUB), :] = low
                    q[k][1, j, pl.ds(row, SUB), :] = high
                if old:
                    tile_cache[j, k] = (low, high, before, after)

    def warm(step, active):
        new_boxes(step * SUB, active, {})

    edges = sorted({-steps(s) for s in lags}) + [0]
    for first, last in zip(edges[:-1], edges[1:]):
        active = [k for k, s in enumerate(lags) if -steps(s) <= first]

        @pl.loop(first, last)
        def _(step, active=active):
            warm(step, active)

    @pl.loop(0, row_count // SUB)
    def _(step):
        base = pl.multiple_of(step * SUB, SUB)
        cache = {"old": True}
        new_boxes(base, range(SCALES), cache)
        east_scale = scale[pl.ds(base, SUB), :]
        for j in range(tiles):
            falling = rising = None
            for k in range(SCALES):
                low, high, old_low, old_high = cache[j, k]
                down, up = old_high - low, high - old_low
                falling = down if falling is None else falling + down
                rising = up if rising is None else rising + up
            results = shade(falling + rising, falling - rising, east_scale)
            for n, value in enumerate(results):
                out[n, pl.ds(base, SUB), j * LANES : (j + 1) * LANES] = value


def load_columns(source, row0, rows, z, z_row0, first, count, sem):
    copies = []
    for j in range(count):
        copies.append(
            pltpu.make_async_copy(
                source.at[pl.ds(row0, rows), j * LANES : (j + 1) * LANES],
                z.at[first + j, pl.ds(z_row0, rows), :],
                sem.at[first + j],
            )
        )
    return copies


def store_rows(out, slope, facing, shading, row0, rows, sem):
    targets = (slope, facing.at[0], facing.at[1], shading)
    return [
        pltpu.make_async_copy(out.at[n], target.at[pl.ds(row0, rows), :], sem.at[n])
        for n, target in enumerate(targets)
    ]


def main_kernel(rows, tiles, where, x, lon, near, scale, slope, facing, shading, *scratch):
    z, out, scale_v, sem_x, sem_near, sem_scale, sem_out = scratch[:7]
    q = scratch[7:]
    odd = where[0]
    own = pl.multiple_of(odd * HALO, HALO)
    beyond = pl.multiple_of((1 - odd) * rows, HALO)
    row0 = pl.multiple_of((1 - odd) * HALO, HALO)
    copies = load_columns(x, 0, rows, z, own, 0, tiles, sem_x)
    copies += load_columns(lon, 0, rows, z, own, tiles, 1, sem_x)
    copies += load_columns(near, 0, HALO, z, beyond, 0, tiles + 1, sem_near)
    copies.append(pltpu.make_async_copy(scale.at[pl.ds(row0, rows - HALO), :], scale_v, sem_scale))
    for copy in copies:
        copy.start()
    for copy in copies:
        copy.wait()
    stencil(z, q, scale_v, out, rows - HALO, tiles)
    stores = store_rows(out, slope, facing, shading, row0, rows - HALO, sem_out)
    for copy in stores:
        copy.start()
    for copy in stores:
        copy.wait()


def rim_kernel(
    rows, tiles, where, x, lon, far, far_lon, scale, _a, _b, _c, slope, facing, shading, *scratch
):
    z, out, scale_v, sem_x, sem_far, sem_scale, sem_out = scratch[:7]
    q = scratch[7:]
    odd, pole = where[0], where[1]
    span = 2 * HALO
    own = pl.multiple_of((1 - odd) * HALO, HALO)
    beyond = pl.multiple_of(odd * span, HALO)
    first = pl.multiple_of(odd * (rows - span), HALO)
    row0 = pl.multiple_of(odd * (rows - HALO), HALO)
    copies = load_columns(x, first, span, z, own, 0, tiles, sem_x)
    copies += load_columns(lon, first, span, z, own, tiles, 1, sem_x)
    copies += load_columns(far, 0, HALO, z, beyond, 0, tiles, sem_far)
    copies += load_columns(far_lon, 0, HALO, z, beyond, tiles, 1, sem_far)
    copies.append(pltpu.make_async_copy(scale.at[pl.ds(row0, HALO), :], scale_v, sem_scale))
    for copy in copies:
        copy.start()
    for copy in copies:
        copy.wait()

    @pl.when(jnp.logical_and(pole == 1, odd == 0))
    def _():
        for j in range(tiles + 1):
            z[j, 0:HALO, :] = jnp.broadcast_to(z[j, HALO : HALO + 1, :], (HALO, LANES))

    @pl.when(jnp.logical_and(pole == 1, odd == 1))
    def _():
        for j in range(tiles + 1):
            z[j, span:, :] = jnp.broadcast_to(z[j, span - 1 : span, :], (HALO, LANES))

    stencil(z, q, scale_v, out, HALO, tiles)
    stores = store_rows(out, slope, facing, shading, row0, HALO, sem_out)
    for copy in stores:
        copy.start()
    for copy in stores:
        copy.wait()


def scratch_for(out_rows, tiles):
    return [
        pltpu.VMEM((tiles + 1, out_rows + 2 * HALO, LANES), jnp.float32),
        pltpu.VMEM((4, out_rows, tiles * LANES), jnp.float32),
        pltpu.VMEM((out_rows, LANES), jnp.float32),
        pltpu.SemaphoreType.DMA((tiles + 1,)),
        pltpu.SemaphoreType.DMA((tiles + 1,)),
        pltpu.SemaphoreType.DMA,
        pltpu.SemaphoreType.DMA((4,)),
    ] + [
        pltpu.VMEM((2, tiles, out_rows + 3 * SUB if 2**k < SUB else 2**k, LANES), jnp.float32)
        for k in range(SCALES)
    ]


def cost(out_rows, cols):
    cells = out_rows * cols
    return pl.CostEstimate(flops=200 * cells, bytes_accessed=24 * cells, transcendentals=3 * cells)


def lon_halo(x):
    count = lax.axis_size("lon")
    first, last = x[:, :HALO], x[:, x.shape[1] - HALO :]
    if count == 2:
        both = jnp.concatenate([first, last], axis=1)
        return lax.ppermute(both, "lon", [(0, 1), (1, 0)])
    westward = [(i, (i - 1) % count) for i in range(count)]
    eastward = [(i, (i + 1) % count) for i in range(count)]
    return jnp.concatenate(
        [lax.ppermute(first, "lon", westward), lax.ppermute(last, "lon", eastward)], axis=1
    )


def pairs(first, count):
    ends = [(i, i + 1) for i in range(first, count - 1, 2)]
    return ends + [(b, a) for a, b in ends]


def local(x):
    rows, cols = x.shape
    tiles = cols // LANES
    lat = lax.axis_index("lat")
    count = lax.axis_size("lat")
    odd = lat % 2
    far_row = odd * (rows - HALO)
    near_row = (1 - odd) * (rows - HALO)

    far = lax.ppermute(lax.dynamic_slice(x, (far_row, 0), (HALO, cols)), "lat", pairs(1, count))
    lon = lon_halo(x)
    near_block = jnp.concatenate(
        [
            lax.dynamic_slice(x, (near_row, 0), (HALO, cols)),
            lax.dynamic_slice(lon, (near_row, 0), (HALO, LANES)),
        ],
        axis=1,
    )
    near = lax.ppermute(near_block, "lat", pairs(0, count))
    far_lon = lax.ppermute(
        lax.dynamic_slice(lon, (far_row, 0), (HALO, LANES)), "lat", pairs(1, count)
    )

    total_rows = rows * count
    total_cols = cols * lax.axis_size("lon")
    position = lat * rows + lax.broadcasted_iota(jnp.int32, (rows, LANES), 0)
    spacing = jnp.sin((position.astype(jnp.float32) + 0.5) * (math.pi / total_rows)) * (
        2.0 * total_rows / total_cols
    )
    scale = -1.0 / (8.0 * SCALES * spacing)
    pole = jnp.logical_or(lat == 0, lat == count - 1)
    where = jnp.stack([odd.astype(jnp.int32), pole.astype(jnp.int32)])

    shapes = [
        jax.ShapeDtypeStruct((rows, cols), jnp.float32),
        jax.ShapeDtypeStruct((2, rows, cols), jnp.float32),
        jax.ShapeDtypeStruct((rows, cols), jnp.float32),
    ]
    smem = pl.BlockSpec(memory_space=pltpu.SMEM)
    anywhere = pl.BlockSpec(memory_space=pl.ANY)
    hbm = pl.BlockSpec(memory_space=pltpu.HBM)
    outs = pl.pallas_call(
        functools.partial(main_kernel, rows, tiles),
        out_shape=shapes,
        in_specs=[smem] + [anywhere] * 4,
        out_specs=[hbm] * 3,
        scratch_shapes=scratch_for(rows - HALO, tiles),
        cost_estimate=cost(rows - HALO, cols),
        compiler_params=pltpu.CompilerParams(vmem_limit_bytes=58 * 2**20),
        name="stencil_main",
    )(where, x, lon, near, scale)
    return tuple(
        pl.pallas_call(
            functools.partial(rim_kernel, rows, tiles),
            out_shape=shapes,
            in_specs=[smem] + [anywhere] * 5 + [hbm] * 3,
            out_specs=[hbm] * 3,
            input_output_aliases={6: 0, 7: 1, 8: 2},
            scratch_shapes=scratch_for(HALO, tiles),
            cost_estimate=cost(HALO, cols),
            compiler_params=pltpu.CompilerParams(vmem_limit_bytes=40 * 2**20),
            name="stencil_rim",
        )(where, x, lon, far, far_lon, scale, *outs)
    )


def solution(mesh):
    in_specs = (P("lat", "lon"),)
    out_specs = (P("lat", "lon"), P(None, "lat", "lon"), P("lat", "lon"))
    return jax.shard_map(local, mesh=mesh, in_specs=in_specs, out_specs=out_specs, check_vma=False)
```

time: 68.3 us -> 42.3 us (0.62)
  the two profiles are of different devices: /device:TPU:9 before, /device:TPU:3 now
where the time goes in v1:
time: 42.3 us; the launch traced here: 42 us
  Pallas kernels  24.4 us (58%)
  starting transfers between devices  9.28 us (22%)
  local copies, waits for them, and re-layouts  4.92 us (12%)
  other arithmetic  1.61 us (4%)
  waiting for transfers between devices  1.05 us (2%)
  between operations  0.75 us (2%)
    pallas_call x1, Pallas kernels, local(): pl.pallas_call(functools.partial(main_kernel, rows, tiles), out_shape=sha...  17.2 us
    pallas_call x1, Pallas kernels, local(): pl.pallas_call(functools.partial(rim_kernel, rows, tiles), out_shape=shap...  7.2 us
    ppermute x1, starting transfers between devices, local(): lax.ppermute(lax.dynamic_slice(lon, (far_row, 0), (HALO, LANES)), 'lat',...  3.27 us
    ppermute x1, starting transfers between devices, local(): lax.ppermute(lax.dynamic_slice(x, (far_row, 0), (HALO, cols)), 'lat', pai...  3.18 us
    dynamic_slice x1, local copies, waits for them, and re-layouts, local(): lax.dynamic_slice(x, (near_row, 0), (HALO, cols))  2.1 us
    ppermute x1, starting transfers between devices, local(): near = lax.ppermute(near_block, 'lat', pairs(0, count))  1.53 us
    ppermute x1, starting transfers between devices, lon_halo(): return lax.ppermute(both, 'lon', [(0, 1), (1, 0)])  1.3 us
    slice x1, local copies, waits for them, and re-layouts, lon_halo(): first, last = (x[:, :HALO], x[:, x.shape[1] - HALO:])  1.06 us
  transfers between devices with their start and end apart: 4, of which 1 were waited for; matrix products, arithmetic and copies ran while one was open for 9% of the time, Pallas kernels for 41%

profile of v1, /device:TPU:3, one launch (start us, length us, event | category | flops | bytes accessed | tf_op | source)
XLA Modules:
  0.0 42.0 jit_solution(2495756168175299276)
XLA Ops:
  0.6 1.1 %fusion = (f32[256,64]{1,0:T(8,128)S(1)}, f32[256,64]{1,0:T(8,128)S(1)}) fusion(f32[256,2048]{1,0:T(8,128)} %x.3), kind=kLoop, calls=%fused_computation.8 | loop fusion | bytes 262144 | tf_op jit(solution)/shard_map/slice | solution.py:230
  1.7 0.1 pad_maximum_fusion.1
  1.8 1.3 %collective-permute-start = (f32[256,128]{1,0:T(8,128)S(1)}, f32[256,128]{1,0:T(8,128)S(1)}, u32[]{:S(2)}, u32[]{:S(2)}) collective-permute-start(f32[256,128]{1,0:T(8,128)S(1)} %pad_maximum_fusion.1), channel_id=1, source_target_pairs={{0,1},{1,0},{2,3},{3,2},{4,5},{5,4},{6,7},{7,6},{8,9},{9,8},{10,11... | collective-permute-start | bytes 393224 | tf_op jit(solution)/shard_map/ppermute | solution.py:233
  3.1 2.1 %constant_dynamic-slice_fusion.1 = (f32[64,2048]{1,0:T(8,128)S(1)}, f32[64,2048]{1,0:T(8,128)}) fusion(f32[256,2048]{1,0:T(8,128)} %x.3, s32[]{:T(128)S(6)} %select_n.17, s32[]{:T(128)S(6)} %select_n.16), kind=kLoop, calls=%fused_computation.4 | loop fusion | bytes 2097160 | tf_op jit(solution)/shard_map/dynamic_slice | solution.py:259
  5.2 1.0 %collective-permute-done.lon = f32[256,128]{1,0:T(8,128)S(1)} collective-permute-done((f32[256,128]{1,0:T(8,128)S(1)}, f32[256,128]{1,0:T(8,128)S(1)}, u32[]{:S(2)}, u32[]{:S(2)}) %collective-permute-start) | collective-permute-done | bytes 131104 | tf_op jit(solution)/shard_map/ppermute | solution.py:233
  6.3 0.0 copy-start
  6.3 0.8 %pad_maximum_fusion = f32[64,2176]{1,0:T(8,128)} fusion(f32[64,128]{1,0:T(8,128)S(1)} %get-tuple-element.13, f32[64,2048]{1,0:T(8,128)S(1)} %get-tuple-element.9), kind=kLoop, calls=%fused_computation | loop fusion | flops 139264 | bytes 1114112 | tf_op jit(solution)/shard_map/concatenate | solution.py:257
  7.1 1.5 %collective-permute-start.3 = (f32[64,2176]{1,0:T(8,128)}, f32[64,2176]{1,0:T(8,128)S(1)}, u32[]{:S(2)}, u32[]{:S(2)}) collective-permute-start(f32[64,2176]{1,0:T(8,128)} %pad_maximum_fusion), channel_id=1, source_target_pairs={{0,2},{4,6},{8,10},{12,14},{16,18},{20,22},{24,26},{28,30},{2,0},{... | collective-permute-start | bytes 1671176 | tf_op jit(solution)/shard_map/ppermute | solution.py:264
  8.7 3.2 %collective-permute-start.1 = (f32[64,2048]{1,0:T(8,128)}, f32[64,2048]{1,0:T(8,128)S(1)}, u32[]{:S(2)}, u32[]{:S(2)}) collective-permute-start(f32[64,2048]{1,0:T(8,128)} %get-tuple-element.10), channel_id=1, source_target_pairs={{2,4},{6,8},{10,12},{14,16},{18,20},{22,24},{26,28},{4,2},{8,6},{1... | collective-permute-start | bytes 1572872 | tf_op jit(solution)/shard_map/ppermute | solution.py:255
  11.9 3.3 %collective-permute-start.2 = (f32[64,128]{1,0:T(8,128)S(1)}, f32[64,128]{1,0:T(8,128)S(1)}, u32[]{:S(2)}, u32[]{:S(2)}) collective-permute-start(f32[64,128]{1,0:T(8,128)S(1)} %get-tuple-element.14), channel_id=1, source_target_pairs={{2,4},{6,8},{10,12},{14,16},{18,20},{22,24},{26,28},{4,2},{8,6},{1... | collective-permute-start | bytes 98312 | tf_op jit(solution)/shard_map/ppermute | solution.py:265
  15.2 0.6 %pad_add_fusion.where = s32[2]{0:T(128)} fusion(s32[1]{0:T(128)} %bitcast.1, s32[1]{0:T(128)} %bitcast), kind=kLoop, calls=%fused_computation.7 | loop fusion | flops 2 | bytes 16 | tf_op jit(solution)/shard_map/stack | solution.py:277
  15.8 0.0 collective-permute-done.3.near
  15.8 0.8 %iota.7.scale = f32[256,128]{1,0:T(8,128)} broadcast(f32[256]{0:T(256)S(1)} %multiply_divide_fusion), dimensions={0} | broadcast | bytes 132096 | tf_op jit(solution)/shard_map/iota | solution.py:271
  16.6 0.0 copy-done.2
  16.6 0.0 copy-done.5
  16.6 17.2 %stencil_main.1 = (f32[256,2048]{1,0:T(8,128)}, f32[2,256,2048]{2,1,0:T(8,128)}, f32[256,2048]{1,0:T(8,128)}) custom-call(s32[2]{0:T(128)} %pad_add_fusion.where, f32[256,2048]{1,0:T(8,128)} %x.3, f32[256,128]{1,0:T(8,128)} %copy-done.2, f32[64,2176]{1,0:T(8,128)} %copy-done.5, f32[256,128]{1,0:T(8,128)} %iota.7.scale), custom_call_target="tpu_custom_call" | custom-call | flops 78643200 | bytes 9437184 | tf_op jit(solution)/shard_map/stencil_main/pallas_call | solution.py:287
  33.9 0.0 collective-permute-done.2.far_lon
  33.9 0.0 collective-permute-done.1.far
  33.9 0.0 copy-done
  33.9 0.0 copy-done.4
  33.9 0.0 copy-done.1
  33.9 0.0 copy-start.3
  33.9 0.9 %copy-done.3 = f32[256,128]{1,0:T(8,128)S(1)} copy-done((f32[256,128]{1,0:T(8,128)S(1)}, f32[256,128]{1,0:T(8,128)}, u32[]{:S(2)}) %copy-start.3) | copy-done | bytes 131096
  34.8 7.2 %stencil_rim.1 = (f32[256,2048]{1,0:T(8,128)}, f32[2,256,2048]{2,1,0:T(8,128)}, f32[256,2048]{1,0:T(8,128)}) custom-call(s32[2]{0:T(128)S(1)} %copy-done.4, f32[256,2048]{1,0:T(8,128)S(1)} %copy-done, f32[256,128]{1,0:T(8,128)S(1)} %copy-done.3, ...), custom_call_target="tpu_custom_call", output_to_operand_aliasing={{0}: (6, {}), {1}: (7, {}), {2}: (8, {})} | custom-call | flops 26214400 | bytes 3145728 | tf_op jit(solution)/shard_map/stencil_rim/pallas_call | solution.py:298
  (6 shorter events, 0.1 us)
Async XLA Ops:
  1.8 4.4 %collective-permute-start = (f32[256,128]{1,0:T(8,128)S(1)}, f32[256,128]{1,0:T(8,128)S(1)}, u32[]{:S(2)}, u32[]{:S(2)}) collective-permute-start(f32[256,128]{1,0:T(8,128)S(1)} %pad_maximum_fusion.1), channel_id=1, source_target_pairs={{0,1},{1,0},{2,3},{3,2},{4,5},{5,4},{6,7},{7,6},{8,9},{9,8},{10,11... | collective-permute-start | bytes 393224 | tf_op jit(solution)/shard_map/ppermute | solution.py:233
  6.3 10.4 %copy-start.2 = (f32[256,128]{1,0:T(8,128)}, f32[256,128]{1,0:T(8,128)S(1)}, u32[]{:S(2)}) copy-start(f32[256,128]{1,0:T(8,128)S(1)} %collective-permute-done.lon) | copy-start | bytes 393220
  6.3 27.6 %copy-start = (f32[256,2048]{1,0:T(8,128)S(1)}, f32[256,2048]{1,0:T(8,128)}, u32[]{:S(2)}) copy-start(f32[256,2048]{1,0:T(8,128)} %x.3) | copy-start | bytes 6291460
  7.1 8.7 %collective-permute-start.3 = (f32[64,2176]{1,0:T(8,128)}, f32[64,2176]{1,0:T(8,128)S(1)}, u32[]{:S(2)}, u32[]{:S(2)}) collective-permute-start(f32[64,2176]{1,0:T(8,128)} %pad_maximum_fusion), channel_id=1, source_target_pairs={{0,2},{4,6},{8,10},{12,14},{16,18},{20,22},{24,26},{28,30},{2,0},{... | collective-permute-start | bytes 1671176 | tf_op jit(solution)/shard_map/ppermute | solution.py:264
  8.7 25.2 %collective-permute-start.1 = (f32[64,2048]{1,0:T(8,128)}, f32[64,2048]{1,0:T(8,128)S(1)}, u32[]{:S(2)}, u32[]{:S(2)}) collective-permute-start(f32[64,2048]{1,0:T(8,128)} %get-tuple-element.10), channel_id=1, source_target_pairs={{2,4},{6,8},{10,12},{14,16},{18,20},{22,24},{26,28},{4,2},{8,6},{1... | collective-permute-start | bytes 1572872 | tf_op jit(solution)/shard_map/ppermute | solution.py:255
  11.9 22.0 %collective-permute-start.2 = (f32[64,128]{1,0:T(8,128)S(1)}, f32[64,128]{1,0:T(8,128)S(1)}, u32[]{:S(2)}, u32[]{:S(2)}) collective-permute-start(f32[64,128]{1,0:T(8,128)S(1)} %get-tuple-element.14), channel_id=1, source_target_pairs={{2,4},{6,8},{10,12},{14,16},{18,20},{22,24},{26,28},{4,2},{8,6},{1... | collective-permute-start | bytes 98312 | tf_op jit(solution)/shard_map/ppermute | solution.py:265
  15.8 18.1 %copy-start.4 = (s32[2]{0:T(128)S(1)}, s32[2]{0:T(128)}, u32[]{:S(2)}) copy-start(s32[2]{0:T(128)} %pad_add_fusion.where) | copy-start | bytes 28
  15.8 0.8 %copy-start.5 = (f32[64,2176]{1,0:T(8,128)}, f32[64,2176]{1,0:T(8,128)S(1)}, u32[]{:S(2)}) copy-start(f32[64,2176]{1,0:T(8,128)S(1)} %collective-permute-done.3.near) | copy-start | bytes 1671172
  16.6 17.3 %copy-start.1 = (f32[256,128]{1,0:T(8,128)S(1)}, f32[256,128]{1,0:T(8,128)}, u32[]{:S(2)}) copy-start(f32[256,128]{1,0:T(8,128)} %iota.7.scale) | copy-start | bytes 393220
  33.9 0.9 %copy-start.3 = (f32[256,128]{1,0:T(8,128)S(1)}, f32[256,128]{1,0:T(8,128)}, u32[]{:S(2)}) copy-start(f32[256,128]{1,0:T(8,128)} %copy-done.2) | copy-start | bytes 393220

commit v2 on v1

v2 whole, which is shorter than its diff:
```python
import functools
import math

import jax
import jax.numpy as jnp
from jax import lax
from jax.experimental import pallas as pl
from jax.experimental.pallas import tpu as pltpu
from jax.sharding import PartitionSpec as P


SCALES = 7
HALO = 64
LANES = 128
SUB = 8
VMEM_LIMIT = 48 * 2**20
HALO_SPACE = pltpu.VMEM

LIGHT_UP = math.sqrt(0.5)
TINY = 1.17549435e-38

SINE_FIT = tuple((-1.0) ** k / math.factorial(2 * k + 1) for k in range(7, -1, -1))
ACOS_FIT = (
    0.036142768221257435,
    -0.1987486877325598,
    0.5130441168137142,
    -0.9077345836840529,
    1.5572964573334291,
)
ANGLE_FIT = tuple(
    c * math.sqrt(2.0) * math.sqrt(0.5) ** (len(ACOS_FIT) - 1 - i) for i, c in enumerate(ACOS_FIT)
)


def shade(east, north, east_scale):
    neg_east = east * east_scale
    neg_north = north * (-1.0 / (8.0 * SCALES))
    squared = neg_east * neg_east + neg_north * neg_north
    inverse = lax.rsqrt(1.0 + squared)
    facing_east = neg_east * inverse
    facing_north = neg_north * inverse
    shading = jnp.maximum(inverse * (0.5 * (neg_north - neg_east) + LIGHT_UP), 0.0)
    sine = squared * lax.rsqrt(jnp.maximum(squared, TINY)) * inverse
    cos_one = 1.0 + inverse
    root = lax.rsqrt(cos_one)
    half = cos_one * root
    fit = ANGLE_FIT[0]
    for coefficient in ANGLE_FIT[1:]:
        fit = fit * half + coefficient
    slope = sine * root * fit
    return slope, facing_east, facing_north, shading


def row_scale(row0, total_rows, total_cols):
    row = row0 + lax.broadcasted_iota(jnp.int32, (SUB, LANES), 0)
    turn = (row.astype(jnp.float32) + 0.5) * (1.0 / total_rows)
    angle = jnp.minimum(turn, 1.0 - turn) * math.pi
    power = angle * angle
    sine = jnp.full_like(angle, SINE_FIT[0])
    for coefficient in SINE_FIT[1:]:
        sine = sine * power + coefficient
    spacing = angle * sine * (2.0 * total_rows / total_cols)
    return -1.0 / (8.0 * SCALES * spacing)


def stencil(z, q, first_row, total, out, held, store, row_count, tiles):
    lane = lax.broadcasted_iota(jnp.int32, (SUB, LANES), 1)
    lags = [2**k for k in range(SCALES)]

    def steps(lag):
        return -(-lag // SUB)

    def new_boxes(base, active, tile_cache):
        here = [z[j, pl.ds(base + HALO, SUB), :] for j in range(tiles + 1)]
        for k in active:
            s = lags[k]
            pairs = []
            for j in range(tiles + 1):
                pair = z[j, pl.ds(base + HALO + s, SUB), :] + here[j]
                pairs.append(pair * (1.0 / s) if k else pair)
            if 2 * s == LANES:
                halves = [
                    pltpu.roll(jnp.where(lane >= s, pairs[j], pairs[(j + 1) % (tiles + 1)]), s, 1)
                    for j in range(tiles + 1)
                ]
            for j in range(tiles):
                before, after = pairs[(j - 1) % (tiles + 1)], pairs[j + 1]
                if 2 * s == LANES:
                    west, east = halves[(j - 1) % (tiles + 1)], halves[j]
                else:
                    west = pltpu.roll(jnp.where(lane < LANES - s, pairs[j], before), s, 1)
                    east = pltpu.roll(jnp.where(lane >= s, pairs[j], after), LANES - s, 1)
                low, high = pairs[j] + west, pairs[j] + east
                old = tile_cache.get("old") is not None
                if s < SUB:
                    q[k][0, j, pl.ds(base + s + SUB, SUB), :] = low
                    q[k][1, j, pl.ds(base + s + SUB, SUB), :] = high
                    if old:
                        before = q[k][0, j, pl.ds(base + SUB, SUB), :]
                        after = q[k][1, j, pl.ds(base + SUB, SUB), :]
                else:
                    slot = lax.bitwise_and(base // SUB, s // SUB - 1)
                    row = pl.multiple_of(slot * SUB, SUB)
                    if old:
                        before = q[k][0, j, pl.ds(row, SUB), :]
                        after = q[k][1, j, pl.ds(row, SUB), :]
                    q[k][0, j, pl.ds(row, SUB), :] = low
                    q[k][1, j, pl.ds(row, SUB), :] = high
                if old:
                    tile_cache[j, k] = (low, high, before, after)

    def warm(step, active):
        new_boxes(step * SUB, active, {})

    edges = sorted({-steps(s) for s in lags}) + [0]
    for first, last in zip(edges[:-1], edges[1:]):
        active = [k for k, s in enumerate(lags) if -steps(s) <= first]

        @pl.loop(first, last)
        def _(step, active=active):
            warm(step, active)

    def sums(step):
        base = pl.multiple_of(step * SUB, SUB)
        cache = {"old": True}
        new_boxes(base, range(SCALES), cache)
        for j in range(tiles):
            falling = rising = None
            for k in range(SCALES):
                low, high, old_low, old_high = cache[j, k]
                down, up = old_high - low, high - old_low
                falling = down if falling is None else falling + down
                rising = up if rising is None else rising + up
            held[0, j] = falling + rising
            held[1, j] = falling - rising

    def finish(step):
        base = pl.multiple_of(step * SUB, SUB)
        east_scale = row_scale(first_row + base, *total)
        for j in range(tiles):
            results = shade(held[0, j], held[1, j], east_scale)
            for n, value in enumerate(results):
                out[n, pl.ds(base, SUB), j * LANES : (j + 1) * LANES] = value

    count = row_count // SUB

    @pl.loop(0, count)
    def _(step):
        finish(jnp.maximum(step - 1, 0))
        sums(step)

        @pl.when(step > 0)
        def _():
            for copy in store(step - 1):
                copy.start()

    finish(count - 1)
    for copy in store(count - 1):
        copy.start()


def column_copies(source, row0, rows, z, z_row0, first, count, sem):
    return [
        pltpu.make_async_copy(
            source.at[pl.ds(row0, rows), j * LANES : (j + 1) * LANES],
            z.at[first + j, pl.ds(z_row0, rows), :],
            sem.at[first + j],
        )
        for j in range(count)
    ]


def row_copies(out, targets, out_row, row0, rows, sem):
    slope, facing, shading = targets
    places = (slope, facing.at[0], facing.at[1], shading)
    return [
        pltpu.make_async_copy(
            out.at[n, pl.ds(out_row, rows), :], place.at[pl.ds(row0, rows), :], sem.at[n]
        )
        for n, place in enumerate(places)
    ]


def run(copies):
    for copy in copies:
        copy.start()
    for copy in copies:
        copy.wait()


def write_rows(z, q, held, out, sem, targets, row0, lat, total, rows, out_rows, tiles):
    def store(step):
        base = pl.multiple_of(step * SUB, SUB)
        return row_copies(out, targets, base, pl.multiple_of(row0 + base, SUB), SUB, sem)

    stencil(z, q, lat * rows + row0, total, out, held, store, out_rows, tiles)
    for copy in row_copies(out, targets, 0, row0, out_rows, sem):
        copy.wait()


def main_kernel(rows, tiles, total, x, lon, near, slope, facing, shading, *scratch):
    z, out, held, sem_x, sem_near, sem_out = scratch[:6]
    lat = lax.axis_index("lat")
    odd = lax.rem(lat, 2)
    own = pl.multiple_of(odd * HALO, HALO)
    beyond = pl.multiple_of((1 - odd) * rows, HALO)
    row0 = pl.multiple_of((1 - odd) * HALO, HALO)
    run(
        column_copies(x, 0, rows, z, own, 0, tiles, sem_x)
        + column_copies(lon, 0, rows, z, own, tiles, 1, sem_x)
        + column_copies(near, 0, HALO, z, beyond, 0, tiles + 1, sem_near)
    )
    write_rows(
        z, scratch[6:], held, out, sem_out, (slope, facing, shading), row0, lat, total, rows,
        rows - HALO, tiles,
    )


def rim_kernel(
    rows, tiles, total, lat_count, x, lon, far, far_lon, _a, _b, _c, slope, facing, shading, *scratch
):
    z, out, held, sem_x, sem_far, sem_out = scratch[:6]
    lat = lax.axis_index("lat")
    odd = lax.rem(lat, 2)
    span = 2 * HALO
    own = pl.multiple_of((1 - odd) * HALO, HALO)
    beyond = pl.multiple_of(odd * span, HALO)
    first = pl.multiple_of(odd * (rows - span), HALO)
    row0 = pl.multiple_of(odd * (rows - HALO), HALO)
    run(
        column_copies(x, first, span, z, own, 0, tiles, sem_x)
        + column_copies(lon, first, span, z, own, tiles, 1, sem_x)
        + column_copies(far, 0, HALO, z, beyond, 0, tiles, sem_far)
        + column_copies(far_lon, 0, HALO, z, beyond, tiles, 1, sem_far)
    )

    @pl.when(lat == 0)
    def _():
        for j in range(tiles + 1):
            z[j, 0:HALO, :] = jnp.broadcast_to(z[j, HALO : HALO + 1, :], (HALO, LANES))

    @pl.when(lat == lat_count - 1)
    def _():
        for j in range(tiles + 1):
            z[j, span:, :] = jnp.broadcast_to(z[j, span - 1 : span, :], (HALO, LANES))

    write_rows(
        z, scratch[6:], held, out, sem_out, (slope, facing, shading), row0, lat, total, rows,
        HALO, tiles,
    )


def scratch_for(out_rows, tiles):
    return [
        pltpu.VMEM((tiles + 1, out_rows + 2 * HALO, LANES), jnp.float32),
        pltpu.VMEM((4, out_rows, tiles * LANES), jnp.float32),
        pltpu.VMEM((2, tiles, SUB, LANES), jnp.float32),
        pltpu.SemaphoreType.DMA((tiles + 1,)),
        pltpu.SemaphoreType.DMA((tiles + 1,)),
        pltpu.SemaphoreType.DMA((4,)),
    ] + [
        pltpu.VMEM((2, tiles, out_rows + 3 * SUB if 2**k < SUB else 2**k, LANES), jnp.float32)
        for k in range(SCALES)
    ]


def cost(out_rows, cols):
    cells = out_rows * cols
    return pl.CostEstimate(flops=200 * cells, bytes_accessed=24 * cells, transcendentals=3 * cells)


def lon_halo(x):
    count = lax.axis_size("lon")
    cols = x.shape[1]
    if count == 2:
        lane = lax.broadcasted_iota(jnp.int32, (x.shape[0], LANES), 1)
        both = jnp.where(lane < HALO, x[:, :LANES], x[:, cols - LANES :])
        return lax.ppermute(both, "lon", [(0, 1), (1, 0)])
    westward = [(i, (i - 1) % count) for i in range(count)]
    eastward = [(i, (i + 1) % count) for i in range(count)]
    east = lax.ppermute(x[:, :HALO], "lon", westward)
    west = lax.ppermute(x[:, cols - HALO :], "lon", eastward)
    return jnp.concatenate([east, west], axis=1)


def pairs(first, count):
    ends = [(i, i + 1) for i in range(first, count - 1, 2)]
    return ends + [(b, a) for a, b in ends]


def local(x):
    rows, cols = x.shape
    tiles = cols // LANES
    lat = lax.axis_index("lat")
    count = lax.axis_size("lat")
    odd = lax.rem(lat, 2)
    far_row = odd * (rows - HALO)
    near_row = (1 - odd) * (rows - HALO)

    far_block = lax.dynamic_slice(x, (far_row, 0), (HALO, cols))
    far = lax.ppermute(far_block, "lat", pairs(1, count))
    lon = lon_halo(x)
    near_block = jnp.concatenate(
        [
            lax.dynamic_slice(x, (near_row, 0), (HALO, cols)),
            lax.dynamic_slice(lon, (near_row, 0), (HALO, LANES)),
        ],
        axis=1,
    )
    near = lax.ppermute(near_block, "lat", pairs(0, count))
    corner_block = lax.dynamic_slice(lon, (far_row, 0), (HALO, LANES))
    far_lon = lax.ppermute(corner_block, "lat", pairs(1, count))

    total = (rows * count, cols * lax.axis_size("lon"))
    shapes = [
        jax.ShapeDtypeStruct((rows, cols), jnp.float32),
        jax.ShapeDtypeStruct((2, rows, cols), jnp.float32),
        jax.ShapeDtypeStruct((rows, cols), jnp.float32),
    ]
    hbm = pl.BlockSpec(memory_space=pltpu.HBM)
    halo = pl.BlockSpec(memory_space=HALO_SPACE)
    outs = pl.pallas_call(
        functools.partial(main_kernel, rows, tiles, total),
        out_shape=shapes,
        in_specs=[hbm, halo, halo],
        out_specs=[hbm] * 3,
        scratch_shapes=scratch_for(rows - HALO, tiles),
        cost_estimate=cost(rows - HALO, cols),
        compiler_params=pltpu.CompilerParams(vmem_limit_bytes=VMEM_LIMIT),
        name="stencil_main",
    )(x, lon, near)
    return tuple(
        pl.pallas_call(
            functools.partial(rim_kernel, rows, tiles, total, count),
            out_shape=shapes,
            in_specs=[hbm] + [halo] * 3 + [hbm] * 3,
            out_specs=[hbm] * 3,
            input_output_aliases={4: 0, 5: 1, 6: 2},
            scratch_shapes=scratch_for(HALO, tiles),
            cost_estimate=cost(HALO, cols),
            compiler_params=pltpu.CompilerParams(vmem_limit_bytes=VMEM_LIMIT),
            name="stencil_rim",
        )(x, lon, far, far_lon, *outs)
    )


def solution(mesh):
    in_specs = (P("lat", "lon"),)
    out_specs = (P("lat", "lon"), P(None, "lat", "lon"), P("lat", "lon"))

    return jax.shard_map(local, mesh=mesh, in_specs=in_specs, out_specs=out_specs, check_vma=False)
```

time: 42.3 us -> 33.3 us (0.79)
  Pallas kernels: 24.4 us -> 18.7 us
  local copies, waits for them, and re-layouts: 4.92 us -> 1.3 us
  waiting for transfers between devices: 1.05 us -> 1.85 us
  other arithmetic: 1.61 us -> 1.18 us
    pallas_call x2, Pallas kernels: 24.4 us -> 18.7 us  [the longest x1 12.8 us: local(): pl.pallas_call(functools.partial(main_kernel, rows, tiles, total), out_sh...]
    select_n x0 -> x1, other arithmetic: none -> 1.13 us  [lon_halo(): both = jnp.where(lane < HALO, x[:, :LANES], x[:, cols - LANES:])]
    slice x1 -> x0, local copies, waits for them, and re-layouts: 1.06 us -> none  [lon_halo(): first, last = (x[:, :HALO], x[:, x.shape[1] - HALO:])]
    unnamed x12 -> x2, local copies, waits for them, and re-layouts: 0.92 us -> 0.01 us
    iota x1 -> x0, local copies, waits for them, and re-layouts: 0.83 us -> none  [local(): position = lat * rows + lax.broadcasted_iota(jnp.int32, (rows, LANES), 0)]
    dynamic_slice x1, local copies, waits for them, and re-layouts: 2.1 us -> 1.29 us  [local(): lax.dynamic_slice(x, (near_row, 0), (HALO, cols))]
    concatenate x1, other arithmetic: 0.84 us -> 0.04 us  [local(): jnp.concatenate([lax.dynamic_slice(x, (near_row, 0), (HALO, cols)), lax.d...]
    ppermute x1, waiting for transfers between devices: 1.04 us -> 1.84 us  [lon_halo(): return lax.ppermute(both, 'lon', [(0, 1), (1, 0)])]
  transfers between devices with their start and end apart: 4 -> 4, of which waited for: 1 -> 1; matrix products, arithmetic and copies ran while one was open for 9% -> 4% of each run, Pallas kernels for 41% -> 39%
where the time goes in v2:
time: 33.3 us; the launch traced here: 33.1 us
  Pallas kernels  18.7 us (56%)
  starting transfers between devices  9.35 us (28%)
  waiting for transfers between devices  1.85 us (6%)
  local copies, waits for them, and re-layouts  1.3 us (4%)
  other arithmetic  1.18 us (4%)
  between operations  0.72 us (2%)
    pallas_call x1, Pallas kernels, local(): pl.pallas_call(functools.partial(main_kernel, rows, tiles, total), out_sh...  12.8 us
    pallas_call x1, Pallas kernels, local(): pl.pallas_call(functools.partial(rim_kernel, rows, tiles, total, count),...  5.93 us
    ppermute x1, starting transfers between devices, local(): far_lon = lax.ppermute(corner_block, 'lat', pairs(1, count))  3.37 us
    ppermute x1, starting transfers between devices, local(): far = lax.ppermute(far_block, 'lat', pairs(1, count))  3.07 us
    ppermute x1, waiting for transfers between devices, lon_halo(): return lax.ppermute(both, 'lon', [(0, 1), (1, 0)])  1.84 us
    ppermute x1, starting transfers between devices, local(): near = lax.ppermute(near_block, 'lat', pairs(0, count))  1.6 us
    ppermute x1, starting transfers between devices, lon_halo(): return lax.ppermute(both, 'lon', [(0, 1), (1, 0)])  1.3 us
    dynamic_slice x1, local copies, waits for them, and re-layouts, local(): lax.dynamic_slice(x, (near_row, 0), (HALO, cols))  1.29 us
  transfers between devices with their start and end apart: 4, of which 1 were waited for; matrix products, arithmetic and copies ran while one was open for 4% of the time, Pallas kernels for 39%

profile of v2, /device:TPU:3, one launch (start us, length us, event | category | flops | bytes accessed | tf_op | source)
XLA Modules:
  0.0 33.1 jit_solution(10622922762757224387)
XLA Ops:
  0.6 0.0 copy-start
  0.7 1.1 %slice_select_fusion = f32[256,128]{1,0:T(8,128)S(1)} fusion(f32[256,2048]{1,0:T(8,128)} %x.3, pred[128]{0:T(512)(128)(4,1)S(1)} %iota_compare_fusion), kind=kLoop, calls=%fused_computation.1 | loop fusion | flops 32768 | bytes 393344 | tf_op jit(solution)/shard_map/jit(_where)/select_n | solution.py:277
  1.8 1.3 %collective-permute-start = (f32[256,128]{1,0:T(8,128)S(1)}, f32[256,128]{1,0:T(8,128)S(1)}, u32[]{:S(2)}, u32[]{:S(2)}) collective-permute-start(f32[256,128]{1,0:T(8,128)S(1)} %slice_select_fusion), channel_id=1, source_target_pairs={{0,1},{1,0},{2,3},{3,2},{4,5},{5,4},{6,7},{7,6},{8,9},{9,8},{10,11... | collective-permute-start | bytes 393224 | tf_op jit(solution)/shard_map/ppermute | solution.py:278
  3.1 1.3 %constant_dynamic-slice_fusion.1 = (f32[64,2048]{1,0:T(8,128)S(1)}, f32[64,2048]{1,0:T(8,128)S(1)}) fusion(f32[256,2048]{1,0:T(8,128)} %x.3, s32[]{:T(128)S(6)} %select_n.14, s32[]{:T(128)S(6)} %select_n.13), kind=kLoop, calls=%fused_computation.3 | loop fusion | bytes 2097160 | tf_op jit(solution)/shard_map/dynamic_slice | solution.py:305
  4.4 1.8 %collective-permute-done.lon = f32[256,128]{1,0:T(8,128)S(1)} collective-permute-done((f32[256,128]{1,0:T(8,128)S(1)}, f32[256,128]{1,0:T(8,128)S(1)}, u32[]{:S(2)}, u32[]{:S(2)}) %collective-permute-start) | collective-permute-done | bytes 131104 | tf_op jit(solution)/shard_map/ppermute | solution.py:278
  6.3 1.6 %collective-permute-start.3 = (f32[64,2176]{1,0:T(8,128)S(1)}, f32[64,2176]{1,0:T(8,128)S(1)}, u32[]{:S(2)}, u32[]{:S(2)}) collective-permute-start(f32[64,2176]{1,0:T(8,128)S(1)} %pad_maximum_fusion), channel_id=1, source_target_pairs={{0,2},{4,6},{8,10},{12,14},{16,18},{20,22},{24,26},{28,30},{2,0},{... | collective-permute-start | bytes 1671176 | tf_op jit(solution)/shard_map/ppermute | solution.py:310
  7.9 3.1 %collective-permute-start.1 = (f32[64,2048]{1,0:T(8,128)S(1)}, f32[64,2048]{1,0:T(8,128)S(1)}, u32[]{:S(2)}, u32[]{:S(2)}) collective-permute-start(f32[64,2048]{1,0:T(8,128)S(1)} %get-tuple-element.10), channel_id=1, source_target_pairs={{2,4},{6,8},{10,12},{14,16},{18,20},{22,24},{26,28},{4,2},{8,6},{1... | collective-permute-start | bytes 1572872 | tf_op jit(solution)/shard_map/ppermute | solution.py:301
  11.0 3.4 %collective-permute-start.2 = (f32[64,128]{1,0:T(8,128)S(1)}, f32[64,128]{1,0:T(8,128)S(1)}, u32[]{:S(2)}, u32[]{:S(2)}) collective-permute-start(f32[64,128]{1,0:T(8,128)S(1)} %get-tuple-element.12), channel_id=1, source_target_pairs={{2,4},{6,8},{10,12},{14,16},{18,20},{22,24},{26,28},{4,2},{8,6},{1... | collective-permute-start | bytes 98312 | tf_op jit(solution)/shard_map/ppermute | solution.py:312
  14.3 0.0 collective-permute-done.3.near
  14.4 0.0 copy-done
  14.4 12.8 %stencil_main.1 = (f32[256,2048]{1,0:T(8,128)}, f32[2,256,2048]{2,1,0:T(8,128)}, f32[256,2048]{1,0:T(8,128)}) custom-call(f32[256,2048]{1,0:T(8,128)S(1)} %copy-done, f32[256,128]{1,0:T(8,128)S(1)} %collective-permute-done.lon, f32[64,2176]{1,0:T(8,128)S(1)} %collective-permute-done.3.near), custom_call_target="tpu_custom_call" | custom-call | flops 78643200 | bytes 9437184 | tf_op jit(solution)/shard_map/stencil_main/pallas_call | solution.py:322
  27.2 0.0 collective-permute-done.2.far_lon
  27.2 0.0 collective-permute-done.1.far
  27.2 5.9 %stencil_rim.1 = (f32[256,2048]{1,0:T(8,128)}, f32[2,256,2048]{2,1,0:T(8,128)}, f32[256,2048]{1,0:T(8,128)}) custom-call(f32[256,2048]{1,0:T(8,128)S(1)} %copy-done, f32[256,128]{1,0:T(8,128)S(1)} %collective-permute-done.lon, f32[64,2048]{1,0:T(8,128)S(1)} %collective-permute-done.1.far, ...), custom_call_target="tpu_custom_call", output_to_operand_aliasing={{0}: (4, {}), {1}: (5, {}), {2}: (6, {})} | custom-call | flops 26214400 | bytes 3145728 | tf_op jit(solution)/shard_map/stencil_rim/pallas_call | solution.py:333
  (3 shorter events, 0.1 us)
Async XLA Ops:
  0.6 13.7 %copy-start = (f32[256,2048]{1,0:T(8,128)S(1)}, f32[256,2048]{1,0:T(8,128)}, u32[]{:S(2)}) copy-start(f32[256,2048]{1,0:T(8,128)} %x.3) | copy-start | bytes 6291460
  1.8 4.4 %collective-permute-start = (f32[256,128]{1,0:T(8,128)S(1)}, f32[256,128]{1,0:T(8,128)S(1)}, u32[]{:S(2)}, u32[]{:S(2)}) collective-permute-start(f32[256,128]{1,0:T(8,128)S(1)} %slice_select_fusion), channel_id=1, source_target_pairs={{0,1},{1,0},{2,3},{3,2},{4,5},{5,4},{6,7},{7,6},{8,9},{9,8},{10,11... | collective-permute-start | bytes 393224 | tf_op jit(solution)/shard_map/ppermute | solution.py:278
  6.3 8.1 %collective-permute-start.3 = (f32[64,2176]{1,0:T(8,128)S(1)}, f32[64,2176]{1,0:T(8,128)S(1)}, u32[]{:S(2)}, u32[]{:S(2)}) collective-permute-start(f32[64,2176]{1,0:T(8,128)S(1)} %pad_maximum_fusion), channel_id=1, source_target_pairs={{0,2},{4,6},{8,10},{12,14},{16,18},{20,22},{24,26},{28,30},{2,0},{... | collective-permute-start | bytes 1671176 | tf_op jit(solution)/shard_map/ppermute | solution.py:310
  7.9 19.3 %collective-permute-start.1 = (f32[64,2048]{1,0:T(8,128)S(1)}, f32[64,2048]{1,0:T(8,128)S(1)}, u32[]{:S(2)}, u32[]{:S(2)}) collective-permute-start(f32[64,2048]{1,0:T(8,128)S(1)} %get-tuple-element.10), channel_id=1, source_target_pairs={{2,4},{6,8},{10,12},{14,16},{18,20},{22,24},{26,28},{4,2},{8,6},{1... | collective-permute-start | bytes 1572872 | tf_op jit(solution)/shard_map/ppermute | solution.py:301
  11.0 16.2 %collective-permute-start.2 = (f32[64,128]{1,0:T(8,128)S(1)}, f32[64,128]{1,0:T(8,128)S(1)}, u32[]{:S(2)}, u32[]{:S(2)}) collective-permute-start(f32[64,128]{1,0:T(8,128)S(1)} %get-tuple-element.12), channel_id=1, source_target_pairs={{2,4},{6,8},{10,12},{14,16},{18,20},{22,24},{26,28},{4,2},{8,6},{1... | collective-permute-start | bytes 98312 | tf_op jit(solution)/shard_map/ppermute | solution.py:312

commit v3 on v2

--- a/solution.py
+++ b/solution.py
@@ -63,7 +63,7 @@
     return -1.0 / (8.0 * SCALES * spacing)
 
 
-def stencil(z, q, first_row, total, out, held, store, row_count, tiles):
+def stencil(z, park, q, first_row, total, out, held, store, row_count, tiles):
     lane = lax.broadcasted_iota(jnp.int32, (SUB, LANES), 1)
     lags = [2**k for k in range(SCALES)]
 
@@ -77,7 +77,9 @@
             pairs = []
             for j in range(tiles + 1):
                 pair = z[j, pl.ds(base + HALO + s, SUB), :] + here[j]
-                pairs.append(pair * (1.0 / s) if k else pair)
+                pair = pair * (1.0 / s) if k else pair
+                park[k, j] = pair
+                pairs.append(pair)
             if 2 * s == LANES:
                 halves = [
                     pltpu.roll(jnp.where(lane >= s, pairs[j], pairs[(j + 1) % (tiles + 1)]), s, 1)
@@ -90,7 +92,7 @@
                 else:
                     west = pltpu.roll(jnp.where(lane < LANES - s, pairs[j], before), s, 1)
                     east = pltpu.roll(jnp.where(lane >= s, pairs[j], after), LANES - s, 1)
-                low, high = pairs[j] + west, pairs[j] + east
+                low, high = park[k, j] + west, park[k, j] + east
                 old = tile_cache.get("old") is not None
                 if s < SUB:
                     q[k][0, j, pl.ds(base + s + SUB, SUB), :] = low
@@ -144,7 +146,7 @@
 
     count = row_count // SUB
 
-    @pl.loop(0, count)
+    @pl.loop(0, count, unroll=2)
     def _(step):
         finish(jnp.maximum(step - 1, 0))
         sums(step)
@@ -188,12 +190,12 @@
         copy.wait()
 
 
-def write_rows(z, q, held, out, sem, targets, row0, lat, total, rows, out_rows, tiles):
+def write_rows(z, park, q, held, out, sem, targets, row0, lat, total, rows, out_rows, tiles):
     def store(step):
         base = pl.multiple_of(step * SUB, SUB)
         return row_copies(out, targets, base, pl.multiple_of(row0 + base, SUB), SUB, sem)
 
-    stencil(z, q, lat * rows + row0, total, out, held, store, out_rows, tiles)
+    stencil(z, park, q, lat * rows + row0, total, out, held, store, out_rows, tiles)
     for copy in row_copies(out, targets, 0, row0, out_rows, sem):
         copy.wait()
 
@@ -211,7 +213,7 @@
         + column_copies(near, 0, HALO, z, beyond, 0, tiles + 1, sem_near)
     )
     write_rows(
-        z, scratch[6:], held, out, sem_out, (slope, facing, shading), row0, lat, total, rows,
+        z, scratch[6], scratch[7:], held, out, sem_out, (slope, facing, shading), row0, lat, total, rows,
         rows - HALO, tiles,
     )
 
@@ -245,7 +247,7 @@
             z[j, span:, :] = jnp.broadcast_to(z[j, span - 1 : span, :], (HALO, LANES))
 
     write_rows(
-        z, scratch[6:], held, out, sem_out, (slope, facing, shading), row0, lat, total, rows,
+        z, scratch[6], scratch[7:], held, out, sem_out, (slope, facing, shading), row0, lat, total, rows,
         HALO, tiles,
     )
 
@@ -258,6 +260,7 @@
         pltpu.SemaphoreType.DMA((tiles + 1,)),
         pltpu.SemaphoreType.DMA((tiles + 1,)),
         pltpu.SemaphoreType.DMA((4,)),
+        pltpu.VMEM((SCALES, tiles + 1, SUB, LANES), jnp.float32),
     ] + [
         pltpu.VMEM((2, tiles, out_rows + 3 * SUB if 2**k < SUB else 2**k, LANES), jnp.float32)
         for k in range(SCALES)

time: 33.3 us -> 31.5 us (0.946)
  Pallas kernels: 18.7 us -> 16.9 us
    pallas_call x1, Pallas kernels: 12.8 us -> 11.4 us  [local(): pl.pallas_call(functools.partial(main_kernel, rows, tiles, total), out_sh...]
    pallas_call x1, Pallas kernels: 5.93 us -> 5.52 us  [local(): pl.pallas_call(functools.partial(rim_kernel, rows, tiles, total, count),...]
  transfers between devices with their start and end apart: 4 -> 4, of which waited for: 1 -> 1; matrix products, arithmetic and copies ran while one was open for 4% -> 4% of each run, Pallas kernels for 39% -> 36%
where the time goes in v3:
time: 31.5 us; the launch traced here: 31.3 us
  Pallas kernels  16.9 us (54%)
  starting transfers between devices  9.35 us (30%)
  waiting for transfers between devices  1.85 us (6%)
  local copies, waits for them, and re-layouts  1.3 us (4%)
  other arithmetic  1.18 us (4%)
  between operations  0.72 us (2%)
    pallas_call x1, Pallas kernels, local(): pl.pallas_call(functools.partial(main_kernel, rows, tiles, total), out_sh...  11.4 us
    pallas_call x1, Pallas kernels, local(): pl.pallas_call(functools.partial(rim_kernel, rows, tiles, total, count),...  5.52 us
    ppermute x1, starting transfers between devices, local(): far_lon = lax.ppermute(corner_block, 'lat', pairs(1, count))  3.37 us
    ppermute x1, starting transfers between devices, local(): far = lax.ppermute(far_block, 'lat', pairs(1, count))  3.07 us
    ppermute x1, waiting for transfers between devices, lon_halo(): return lax.ppermute(both, 'lon', [(0, 1), (1, 0)])  1.84 us
    ppermute x1, starting transfers between devices, local(): near = lax.ppermute(near_block, 'lat', pairs(0, count))  1.6 us
    ppermute x1, starting transfers between devices, lon_halo(): return lax.ppermute(both, 'lon', [(0, 1), (1, 0)])  1.3 us
    dynamic_slice x1, local copies, waits for them, and re-layouts, local(): lax.dynamic_slice(x, (near_row, 0), (HALO, cols))  1.29 us
  transfers between devices with their start and end apart: 4, of which 1 were waited for; matrix products, arithmetic and copies ran while one was open for 4% of the time, Pallas kernels for 36%

profile of v3, /device:TPU:3, one launch (start us, length us, event | category | flops | bytes accessed | tf_op | source)
XLA Modules:
  0.0 31.3 jit_solution(13599082027703999454)
XLA Ops:
  0.6 0.0 copy-start
  0.7 1.1 %slice_select_fusion = f32[256,128]{1,0:T(8,128)S(1)} fusion(f32[256,2048]{1,0:T(8,128)} %x.3, pred[128]{0:T(512)(128)(4,1)S(1)} %iota_compare_fusion), kind=kLoop, calls=%fused_computation.1 | loop fusion | flops 32768 | bytes 393344 | tf_op jit(solution)/shard_map/jit(_where)/select_n | solution.py:280
  1.8 1.3 %collective-permute-start = (f32[256,128]{1,0:T(8,128)S(1)}, f32[256,128]{1,0:T(8,128)S(1)}, u32[]{:S(2)}, u32[]{:S(2)}) collective-permute-start(f32[256,128]{1,0:T(8,128)S(1)} %slice_select_fusion), channel_id=1, source_target_pairs={{0,1},{1,0},{2,3},{3,2},{4,5},{5,4},{6,7},{7,6},{8,9},{9,8},{10,11... | collective-permute-start | bytes 393224 | tf_op jit(solution)/shard_map/ppermute | solution.py:281
  3.1 1.3 %constant_dynamic-slice_fusion.1 = (f32[64,2048]{1,0:T(8,128)S(1)}, f32[64,2048]{1,0:T(8,128)S(1)}) fusion(f32[256,2048]{1,0:T(8,128)} %x.3, s32[]{:T(128)S(6)} %select_n.14, s32[]{:T(128)S(6)} %select_n.13), kind=kLoop, calls=%fused_computation.3 | loop fusion | bytes 2097160 | tf_op jit(solution)/shard_map/dynamic_slice | solution.py:308
  4.4 1.8 %collective-permute-done.lon = f32[256,128]{1,0:T(8,128)S(1)} collective-permute-done((f32[256,128]{1,0:T(8,128)S(1)}, f32[256,128]{1,0:T(8,128)S(1)}, u32[]{:S(2)}, u32[]{:S(2)}) %collective-permute-start) | collective-permute-done | bytes 131104 | tf_op jit(solution)/shard_map/ppermute | solution.py:281
  6.3 1.6 %collective-permute-start.3 = (f32[64,2176]{1,0:T(8,128)S(1)}, f32[64,2176]{1,0:T(8,128)S(1)}, u32[]{:S(2)}, u32[]{:S(2)}) collective-permute-start(f32[64,2176]{1,0:T(8,128)S(1)} %pad_maximum_fusion), channel_id=1, source_target_pairs={{0,2},{4,6},{8,10},{12,14},{16,18},{20,22},{24,26},{28,30},{2,0},{... | collective-permute-start | bytes 1671176 | tf_op jit(solution)/shard_map/ppermute | solution.py:313
  7.9 3.1 %collective-permute-start.1 = (f32[64,2048]{1,0:T(8,128)S(1)}, f32[64,2048]{1,0:T(8,128)S(1)}, u32[]{:S(2)}, u32[]{:S(2)}) collective-permute-start(f32[64,2048]{1,0:T(8,128)S(1)} %get-tuple-element.10), channel_id=1, source_target_pairs={{2,4},{6,8},{10,12},{14,16},{18,20},{22,24},{26,28},{4,2},{8,6},{1... | collective-permute-start | bytes 1572872 | tf_op jit(solution)/shard_map/ppermute | solution.py:304
  11.0 3.4 %collective-permute-start.2 = (f32[64,128]{1,0:T(8,128)S(1)}, f32[64,128]{1,0:T(8,128)S(1)}, u32[]{:S(2)}, u32[]{:S(2)}) collective-permute-start(f32[64,128]{1,0:T(8,128)S(1)} %get-tuple-element.12), channel_id=1, source_target_pairs={{2,4},{6,8},{10,12},{14,16},{18,20},{22,24},{26,28},{4,2},{8,6},{1... | collective-permute-start | bytes 98312 | tf_op jit(solution)/shard_map/ppermute | solution.py:315
  14.3 0.0 collective-permute-done.3.near
  14.4 0.0 copy-done
  14.4 11.4 %stencil_main.1 = (f32[256,2048]{1,0:T(8,128)}, f32[2,256,2048]{2,1,0:T(8,128)}, f32[256,2048]{1,0:T(8,128)}) custom-call(f32[256,2048]{1,0:T(8,128)S(1)} %copy-done, f32[256,128]{1,0:T(8,128)S(1)} %collective-permute-done.lon, f32[64,2176]{1,0:T(8,128)S(1)} %collective-permute-done.3.near), custom_call_target="tpu_custom_call" | custom-call | flops 78643200 | bytes 9437184 | tf_op jit(solution)/shard_map/stencil_main/pallas_call | solution.py:325
  25.8 0.0 collective-permute-done.2.far_lon
  25.8 0.0 collective-permute-done.1.far
  25.8 5.5 %stencil_rim.1 = (f32[256,2048]{1,0:T(8,128)}, f32[2,256,2048]{2,1,0:T(8,128)}, f32[256,2048]{1,0:T(8,128)}) custom-call(f32[256,2048]{1,0:T(8,128)S(1)} %copy-done, f32[256,128]{1,0:T(8,128)S(1)} %collective-permute-done.lon, f32[64,2048]{1,0:T(8,128)S(1)} %collective-permute-done.1.far, ...), custom_call_target="tpu_custom_call", output_to_operand_aliasing={{0}: (4, {}), {1}: (5, {}), {2}: (6, {})} | custom-call | flops 26214400 | bytes 3145728 | tf_op jit(solution)/shard_map/stencil_rim/pallas_call | solution.py:336
  (3 shorter events, 0.1 us)
Async XLA Ops:
  0.6 13.7 %copy-start = (f32[256,2048]{1,0:T(8,128)S(1)}, f32[256,2048]{1,0:T(8,128)}, u32[]{:S(2)}) copy-start(f32[256,2048]{1,0:T(8,128)} %x.3) | copy-start | bytes 6291460
  1.8 4.4 %collective-permute-start = (f32[256,128]{1,0:T(8,128)S(1)}, f32[256,128]{1,0:T(8,128)S(1)}, u32[]{:S(2)}, u32[]{:S(2)}) collective-permute-start(f32[256,128]{1,0:T(8,128)S(1)} %slice_select_fusion), channel_id=1, source_target_pairs={{0,1},{1,0},{2,3},{3,2},{4,5},{5,4},{6,7},{7,6},{8,9},{9,8},{10,11... | collective-permute-start | bytes 393224 | tf_op jit(solution)/shard_map/ppermute | solution.py:281
  6.3 8.1 %collective-permute-start.3 = (f32[64,2176]{1,0:T(8,128)S(1)}, f32[64,2176]{1,0:T(8,128)S(1)}, u32[]{:S(2)}, u32[]{:S(2)}) collective-permute-start(f32[64,2176]{1,0:T(8,128)S(1)} %pad_maximum_fusion), channel_id=1, source_target_pairs={{0,2},{4,6},{8,10},{12,14},{16,18},{20,22},{24,26},{28,30},{2,0},{... | collective-permute-start | bytes 1671176 | tf_op jit(solution)/shard_map/ppermute | solution.py:313
  7.9 17.9 %collective-permute-start.1 = (f32[64,2048]{1,0:T(8,128)S(1)}, f32[64,2048]{1,0:T(8,128)S(1)}, u32[]{:S(2)}, u32[]{:S(2)}) collective-permute-start(f32[64,2048]{1,0:T(8,128)S(1)} %get-tuple-element.10), channel_id=1, source_target_pairs={{2,4},{6,8},{10,12},{14,16},{18,20},{22,24},{26,28},{4,2},{8,6},{1... | collective-permute-start | bytes 1572872 | tf_op jit(solution)/shard_map/ppermute | solution.py:304
  11.0 14.8 %collective-permute-start.2 = (f32[64,128]{1,0:T(8,128)S(1)}, f32[64,128]{1,0:T(8,128)S(1)}, u32[]{:S(2)}, u32[]{:S(2)}) collective-permute-start(f32[64,128]{1,0:T(8,128)S(1)} %get-tuple-element.12), channel_id=1, source_target_pairs={{2,4},{6,8},{10,12},{14,16},{18,20},{22,24},{26,28},{4,2},{8,6},{1... | collective-permute-start | bytes 98312 | tf_op jit(solution)/shard_map/ppermute | solution.py:315

commit v4 on v3

--- a/solution.py
+++ b/solution.py
@@ -146,7 +146,7 @@
 
     count = row_count // SUB
 
-    @pl.loop(0, count, unroll=2)
+    @pl.loop(0, count, unroll=4)
     def _(step):
         finish(jnp.maximum(step - 1, 0))
         sums(step)
@@ -172,6 +172,14 @@
     ]
 
 
+def tile_copy(source, row0, rows, z, z_row0, tile, sem):
+    return pltpu.make_async_copy(
+        source.at[pl.ds(pl.multiple_of(row0, HALO), rows), :],
+        z.at[tile, pl.ds(pl.multiple_of(z_row0, HALO), rows), :],
+        sem,
+    )
+
+
 def row_copies(out, targets, out_row, row0, rows, sem):
     slope, facing, shading = targets
     places = (slope, facing.at[0], facing.at[1], shading)
@@ -200,28 +208,34 @@
         copy.wait()
 
 
-def main_kernel(rows, tiles, total, x, lon, near, slope, facing, shading, *scratch):
-    z, out, held, sem_x, sem_near, sem_out = scratch[:6]
+def main_kernel(rows, tiles, total, x, lon_rim, lon_mid, near, slope, facing, shading, *scratch):
+    z, out, held, sem_x, sem_lon, sem_near, sem_out = scratch[:7]
     lat = lax.axis_index("lat")
     odd = lax.rem(lat, 2)
     own = pl.multiple_of(odd * HALO, HALO)
     beyond = pl.multiple_of((1 - odd) * rows, HALO)
     row0 = pl.multiple_of((1 - odd) * HALO, HALO)
+    mid = rows - 2 * HALO
     run(
         column_copies(x, 0, rows, z, own, 0, tiles, sem_x)
-        + column_copies(lon, 0, rows, z, own, tiles, 1, sem_x)
+        + [
+            tile_copy(lon_rim, 0, HALO, z, own, tiles, sem_lon.at[0]),
+            tile_copy(lon_mid, 0, mid, z, own + HALO, tiles, sem_lon.at[1]),
+            tile_copy(lon_rim, HALO, HALO, z, own + HALO + mid, tiles, sem_lon.at[2]),
+        ]
         + column_copies(near, 0, HALO, z, beyond, 0, tiles + 1, sem_near)
     )
     write_rows(
-        z, scratch[6], scratch[7:], held, out, sem_out, (slope, facing, shading), row0, lat, total, rows,
-        rows - HALO, tiles,
+        z, scratch[7], scratch[8:], held, out, sem_out, (slope, facing, shading), row0, lat, total,
+        rows, rows - HALO, tiles,
     )
 
 
 def rim_kernel(
-    rows, tiles, total, lat_count, x, lon, far, far_lon, _a, _b, _c, slope, facing, shading, *scratch
+    rows, tiles, total, lat_count, x, lon_rim, lon_mid, far, _a, _b, _c, slope, facing, shading,
+    *scratch,
 ):
-    z, out, held, sem_x, sem_far, sem_out = scratch[:6]
+    z, out, held, sem_x, sem_lon, sem_far, sem_out = scratch[:7]
     lat = lax.axis_index("lat")
     odd = lax.rem(lat, 2)
     span = 2 * HALO
@@ -229,11 +243,15 @@
     beyond = pl.multiple_of(odd * span, HALO)
     first = pl.multiple_of(odd * (rows - span), HALO)
     row0 = pl.multiple_of(odd * (rows - HALO), HALO)
+    edge = pl.multiple_of(odd * HALO, HALO)
+    mid = pl.multiple_of(odd * (rows - 3 * HALO), HALO)
     run(
         column_copies(x, first, span, z, own, 0, tiles, sem_x)
-        + column_copies(lon, first, span, z, own, tiles, 1, sem_x)
-        + column_copies(far, 0, HALO, z, beyond, 0, tiles, sem_far)
-        + column_copies(far_lon, 0, HALO, z, beyond, tiles, 1, sem_far)
+        + [
+            tile_copy(lon_rim, edge, HALO, z, own + edge, tiles, sem_lon.at[0]),
+            tile_copy(lon_mid, mid, HALO, z, own + HALO - edge, tiles, sem_lon.at[1]),
+        ]
+        + column_copies(far, 0, HALO, z, beyond, 0, tiles + 1, sem_far)
     )
 
     @pl.when(lat == 0)
@@ -247,8 +265,8 @@
             z[j, span:, :] = jnp.broadcast_to(z[j, span - 1 : span, :], (HALO, LANES))
 
     write_rows(
-        z, scratch[6], scratch[7:], held, out, sem_out, (slope, facing, shading), row0, lat, total, rows,
-        HALO, tiles,
+        z, scratch[7], scratch[8:], held, out, sem_out, (slope, facing, shading), row0, lat, total,
+        rows, HALO, tiles,
     )
 
 
@@ -257,7 +275,8 @@
         pltpu.VMEM((tiles + 1, out_rows + 2 * HALO, LANES), jnp.float32),
         pltpu.VMEM((4, out_rows, tiles * LANES), jnp.float32),
         pltpu.VMEM((2, tiles, SUB, LANES), jnp.float32),
-        pltpu.SemaphoreType.DMA((tiles + 1,)),
+        pltpu.SemaphoreType.DMA((tiles,)),
+        pltpu.SemaphoreType.DMA((3,)),
         pltpu.SemaphoreType.DMA((tiles + 1,)),
         pltpu.SemaphoreType.DMA((4,)),
         pltpu.VMEM((SCALES, tiles + 1, SUB, LANES), jnp.float32),
@@ -272,17 +291,16 @@
     return pl.CostEstimate(flops=200 * cells, bytes_accessed=24 * cells, transcendentals=3 * cells)
 
 
-def lon_halo(x):
+def lon_halo(first, last):
     count = lax.axis_size("lon")
-    cols = x.shape[1]
     if count == 2:
-        lane = lax.broadcasted_iota(jnp.int32, (x.shape[0], LANES), 1)
-        both = jnp.where(lane < HALO, x[:, :LANES], x[:, cols - LANES :])
+        lane = lax.broadcasted_iota(jnp.int32, first.shape, 1)
+        both = jnp.where(lane < HALO, first, last)
         return lax.ppermute(both, "lon", [(0, 1), (1, 0)])
     westward = [(i, (i - 1) % count) for i in range(count)]
     eastward = [(i, (i + 1) % count) for i in range(count)]
-    east = lax.ppermute(x[:, :HALO], "lon", westward)
-    west = lax.ppermute(x[:, cols - HALO :], "lon", eastward)
+    east = lax.ppermute(first[:, :HALO], "lon", westward)
+    west = lax.ppermute(last[:, LANES - HALO :], "lon", eastward)
     return jnp.concatenate([east, west], axis=1)
 
 
@@ -297,22 +315,24 @@
     lat = lax.axis_index("lat")
     count = lax.axis_size("lat")
     odd = lax.rem(lat, 2)
-    far_row = odd * (rows - HALO)
-    near_row = (1 - odd) * (rows - HALO)
-
-    far_block = lax.dynamic_slice(x, (far_row, 0), (HALO, cols))
-    far = lax.ppermute(far_block, "lat", pairs(1, count))
-    lon = lon_halo(x)
-    near_block = jnp.concatenate(
-        [
-            lax.dynamic_slice(x, (near_row, 0), (HALO, cols)),
-            lax.dynamic_slice(lon, (near_row, 0), (HALO, LANES)),
-        ],
-        axis=1,
-    )
-    near = lax.ppermute(near_block, "lat", pairs(0, count))
-    corner_block = lax.dynamic_slice(lon, (far_row, 0), (HALO, LANES))
-    far_lon = lax.ppermute(corner_block, "lat", pairs(1, count))
+
+    def both_rims(part):
+        return jnp.concatenate([part[:HALO], part[rows - HALO :]], axis=0)
+
+    def rim(start):
+        return jnp.concatenate(
+            [
+                lax.dynamic_slice(x, (start * (rows - HALO), 0), (HALO, cols)),
+                lax.dynamic_slice(lon_rim, (start * HALO, 0), (HALO, LANES)),
+            ],
+            axis=1,
+        )
+
+    first, last = x[:, :LANES], x[:, cols - LANES :]
+    lon_rim = lon_halo(both_rims(first), both_rims(last))
+    lon_mid = lon_halo(first[HALO : rows - HALO], last[HALO : rows - HALO])
+    far = lax.ppermute(rim(odd), "lat", pairs(1, count))
+    near = lax.ppermute(rim(1 - odd), "lat", pairs(0, count))
 
     total = (rows * count, cols * lax.axis_size("lon"))
     shapes = [
@@ -325,13 +345,13 @@
     outs = pl.pallas_call(
         functools.partial(main_kernel, rows, tiles, total),
         out_shape=shapes,
-        in_specs=[hbm, halo, halo],
+        in_specs=[hbm] + [halo] * 3,
         out_specs=[hbm] * 3,
         scratch_shapes=scratch_for(rows - HALO, tiles),
         cost_estimate=cost(rows - HALO, cols),
         compiler_params=pltpu.CompilerParams(vmem_limit_bytes=VMEM_LIMIT),
         name="stencil_main",
-    )(x, lon, near)
+    )(x, lon_rim, lon_mid, near)
     return tuple(
         pl.pallas_call(
             functools.partial(rim_kernel, rows, tiles, total, count),
@@ -343,7 +363,7 @@
             cost_estimate=cost(HALO, cols),
             compiler_params=pltpu.CompilerParams(vmem_limit_bytes=VMEM_LIMIT),
             name="stencil_rim",
-        )(x, lon, far, far_lon, *outs)
+        )(x, lon_rim, lon_mid, far, *outs)
     )
 
 

time: 31.5 us -> 31.2 us (level)
  the two profiles are of different devices: /device:TPU:3 before, /device:TPU:7 now
where the time goes in v4:
time: 31.2 us; the launch traced here: 31 us
  Pallas kernels  16.2 us (52%)
  starting transfers between devices  5.55 us (18%)
  waiting for transfers between devices  5.28 us (17%)
  local copies, waits for them, and re-layouts  2.25 us (7%)
  other arithmetic  0.98 us (3%)
  between operations  0.69 us (2%)
    pallas_call x1, Pallas kernels, local(): pl.pallas_call(functools.partial(main_kernel, rows, tiles, total), out_sh...  10.9 us
    pallas_call x1, Pallas kernels, local(): pl.pallas_call(functools.partial(rim_kernel, rows, tiles, total, count),...  5.3 us
    ppermute x2, waiting for transfers between devices, lon_halo(): return lax.ppermute(both, 'lon', [(0, 1), (1, 0)])  5.27 us
    ppermute x1, starting transfers between devices, local(): far = lax.ppermute(rim(odd), 'lat', pairs(1, count))  3.08 us
    ppermute x1, starting transfers between devices, local(): near = lax.ppermute(rim(1 - odd), 'lat', pairs(0, count))  1.89 us
    dynamic_slice x1, local copies, waits for them, and re-layouts, rim(): lax.dynamic_slice(x, (start * (rows - HALO), 0), (HALO, cols))  1.42 us
    select_n x1, other arithmetic, lon_halo(): both = jnp.where(lane < HALO, first, last)  0.9 us
    slice x1, local copies, waits for them, and re-layouts, both_rims(): return jnp.concatenate([part[:HALO], part[rows - HALO:]], axis=0)  0.82 us
  transfers between devices with their start and end apart: 4, of which 2 were waited for; matrix products, arithmetic and copies ran while one was open for 5% of the time, Pallas kernels for 35%

profile of v4, /device:TPU:7, one launch (start us, length us, event | category | flops | bytes accessed | tf_op | source)
XLA Modules:
  0.0 31.0 jit_solution(14201181573967197309)
XLA Ops:
  0.6 0.8 %fusion = (f32[64,128]{1,0:T(8,128)S(1)}, f32[64,128]{1,0:T(8,128)S(1)}, f32[64,128]{1,0:T(8,128)S(1)}, f32[64,128]{1,0:T(8,128)S(1)}) fusion(f32[256,2048]{1,0:T(8,128)} %x.3), kind=kLoop, calls=%fused_computation.9 | loop fusion | bytes 262144 | tf_op jit(solution)/shard_map/slice | solution.py:320
  1.5 0.9 %slice_select_fusion = (f32[128,128]{1,0:T(8,128)S(1)}, f32[128,128]{1,0:T(8,128)S(1)}) fusion(f32[256,2048]{1,0:T(8,128)} %x.3, pred[128]{0:T(512)(128)(4,1)S(1)} %iota_compare_fusion, f32[64,128]{1,0:T(8,128)S(1)} %get-tuple-element.12, f32[64,128]{1,0:T(8,128)S(1)} %get-tuple-element.11, f32[64,128]{1,0:T(8,128)S(1)} %get-tuple-element.13, ...), kind=kLoop, calls=%fused_computation.3 | loop fusion | flops 65536 | bytes 393344 | tf_op jit(solution)/shard_map/jit(_where)/select_n | solution.py:298
  2.4 0.3 collective-permute-start
  2.7 0.0 copy-start
  2.7 1.4 %constant_dynamic-slice_fusion.1 = (f32[64,2048]{1,0:T(8,128)S(1)}, f32[64,2048]{1,0:T(8,128)S(1)}) fusion(f32[256,2048]{1,0:T(8,128)} %x.3, s32[]{:T(128)S(6)} %select_n.23, s32[]{:T(128)S(6)} %select_n.21), kind=kLoop, calls=%fused_computation.5 | loop fusion | bytes 2097160 | tf_op jit(solution)/shard_map/dynamic_slice | solution.py:325
  4.1 1.5 %collective-permute-done.lon_rim = f32[128,128]{1,0:T(8,128)S(1)} collective-permute-done((f32[128,128]{1,0:T(8,128)S(1)}, f32[128,128]{1,0:T(8,128)S(1)}, u32[]{:S(2)}, u32[]{:S(2)}) %collective-permute-start) | collective-permute-done | bytes 65568 | tf_op jit(solution)/shard_map/ppermute | solution.py:299
  5.6 1.9 %collective-permute-start.3 = (f32[64,2176]{1,0:T(8,128)S(1)}, f32[64,2176]{1,0:T(8,128)S(1)}, u32[]{:S(2)}, u32[]{:S(2)}) collective-permute-start(f32[64,2176]{1,0:T(8,128)S(1)} %pad_maximum_fusion.1), channel_id=1, source_target_pairs={{0,2},{4,6},{8,10},{12,14},{16,18},{20,22},{24,26},{28,30},{2,0},{... | collective-permute-start | bytes 1671176 | tf_op jit(solution)/shard_map/ppermute | solution.py:335
  7.5 3.1 %collective-permute-start.2 = (f32[64,2176]{1,0:T(8,128)S(1)}, f32[64,2176]{1,0:T(8,128)S(1)}, u32[]{:S(2)}, u32[]{:S(2)}) collective-permute-start(f32[64,2176]{1,0:T(8,128)S(1)} %pad_maximum_fusion), channel_id=1, source_target_pairs={{2,4},{6,8},{10,12},{14,16},{18,20},{22,24},{26,28},{4,2},{8,6},{1... | collective-permute-start | bytes 1671176 | tf_op jit(solution)/shard_map/ppermute | solution.py:334
  10.6 0.3 collective-permute-start.1
  10.9 3.8 %collective-permute-done.1.lon_mid = f32[128,128]{1,0:T(8,128)S(1)} collective-permute-done((f32[128,128]{1,0:T(8,128)S(1)}, f32[128,128]{1,0:T(8,128)S(1)}, u32[]{:S(2)}, u32[]{:S(2)}) %collective-permute-start.1) | collective-permute-done | bytes 65568 | tf_op jit(solution)/shard_map/ppermute | solution.py:299
  14.7 0.0 collective-permute-done.3.near
  14.7 0.0 copy-done
  14.7 10.9 %stencil_main.1 = (f32[256,2048]{1,0:T(8,128)}, f32[2,256,2048]{2,1,0:T(8,128)}, f32[256,2048]{1,0:T(8,128)}) custom-call(f32[256,2048]{1,0:T(8,128)S(1)} %copy-done, f32[128,128]{1,0:T(8,128)S(1)} %collective-permute-done.lon_rim, f32[128,128]{1,0:T(8,128)S(1)} %collective-permute-done.1.lon_mid, f32[64,2176]{1,0:T(8,128)S(1)} %collective-permute-done.3.near), custom_call_target="tpu_custom_call" | custom-call | flops 78643200 | bytes 9437184 | tf_op jit(solution)/shard_map/stencil_main/pallas_call | solution.py:345
  25.6 0.0 collective-permute-done.2.far
  25.6 5.3 %stencil_rim.1 = (f32[256,2048]{1,0:T(8,128)}, f32[2,256,2048]{2,1,0:T(8,128)}, f32[256,2048]{1,0:T(8,128)}) custom-call(f32[256,2048]{1,0:T(8,128)S(1)} %copy-done, f32[128,128]{1,0:T(8,128)S(1)} %collective-permute-done.lon_rim, f32[128,128]{1,0:T(8,128)S(1)} %collective-permute-done.1.lon_mid, ...), custom_call_target="tpu_custom_call", output_to_operand_aliasing={{0}: (4, {}), {1}: (5, {}), {2}: (6, {})} | custom-call | flops 26214400 | bytes 3145728 | tf_op jit(solution)/shard_map/stencil_rim/pallas_call | solution.py:356
  (4 shorter events, 0.1 us)
Async XLA Ops:
  2.4 3.2 %collective-permute-start = (f32[128,128]{1,0:T(8,128)S(1)}, f32[128,128]{1,0:T(8,128)S(1)}, u32[]{:S(2)}, u32[]{:S(2)}) collective-permute-start(f32[128,128]{1,0:T(8,128)S(1)} %get-tuple-element.18), channel_id=1, source_target_pairs={{0,1},{1,0},{2,3},{3,2},{4,5},{5,4},{6,7},{7,6},{8,9},{9,8},{10,11... | collective-permute-start | bytes 196616 | tf_op jit(solution)/shard_map/ppermute | solution.py:299
  2.7 12.1 %copy-start = (f32[256,2048]{1,0:T(8,128)S(1)}, f32[256,2048]{1,0:T(8,128)}, u32[]{:S(2)}) copy-start(f32[256,2048]{1,0:T(8,128)} %x.3) | copy-start | bytes 6291460
  5.6 9.1 %collective-permute-start.3 = (f32[64,2176]{1,0:T(8,128)S(1)}, f32[64,2176]{1,0:T(8,128)S(1)}, u32[]{:S(2)}, u32[]{:S(2)}) collective-permute-start(f32[64,2176]{1,0:T(8,128)S(1)} %pad_maximum_fusion.1), channel_id=1, source_target_pairs={{0,2},{4,6},{8,10},{12,14},{16,18},{20,22},{24,26},{28,30},{2,0},{... | collective-permute-start | bytes 1671176 | tf_op jit(solution)/shard_map/ppermute | solution.py:335
  7.5 18.1 %collective-permute-start.2 = (f32[64,2176]{1,0:T(8,128)S(1)}, f32[64,2176]{1,0:T(8,128)S(1)}, u32[]{:S(2)}, u32[]{:S(2)}) collective-permute-start(f32[64,2176]{1,0:T(8,128)S(1)} %pad_maximum_fusion), channel_id=1, source_target_pairs={{2,4},{6,8},{10,12},{14,16},{18,20},{22,24},{26,28},{4,2},{8,6},{1... | collective-permute-start | bytes 1671176 | tf_op jit(solution)/shard_map/ppermute | solution.py:334
  10.6 4.1 %collective-permute-start.1 = (f32[128,128]{1,0:T(8,128)S(1)}, f32[128,128]{1,0:T(8,128)S(1)}, u32[]{:S(2)}, u32[]{:S(2)}) collective-permute-start(f32[128,128]{1,0:T(8,128)S(1)} %get-tuple-element.17), channel_id=1, source_target_pairs={{0,1},{1,0},{2,3},{3,2},{4,5},{5,4},{6,7},{7,6},{8,9},{9,8},{10,11... | collective-permute-start | bytes 196616 | tf_op jit(solution)/shard_map/ppermute | solution.py:299

commit v5 on v3

--- a/solution.py
+++ b/solution.py
@@ -118,7 +118,7 @@
     for first, last in zip(edges[:-1], edges[1:]):
         active = [k for k, s in enumerate(lags) if -steps(s) <= first]
 
-        @pl.loop(first, last)
+        @pl.loop(first, last, unroll=last - first)
         def _(step, active=active):
             warm(step, active)
 
@@ -146,7 +146,7 @@
 
     count = row_count // SUB
 
-    @pl.loop(0, count, unroll=2)
+    @pl.loop(0, count, unroll=4)
     def _(step):
         finish(jnp.maximum(step - 1, 0))
         sums(step)
@@ -272,17 +272,14 @@
     return pl.CostEstimate(flops=200 * cells, bytes_accessed=24 * cells, transcendentals=3 * cells)
 
 
-def lon_halo(x):
+def lon_halo(sides):
     count = lax.axis_size("lon")
-    cols = x.shape[1]
     if count == 2:
-        lane = lax.broadcasted_iota(jnp.int32, (x.shape[0], LANES), 1)
-        both = jnp.where(lane < HALO, x[:, :LANES], x[:, cols - LANES :])
-        return lax.ppermute(both, "lon", [(0, 1), (1, 0)])
+        return lax.ppermute(sides, "lon", [(0, 1), (1, 0)])
     westward = [(i, (i - 1) % count) for i in range(count)]
     eastward = [(i, (i + 1) % count) for i in range(count)]
-    east = lax.ppermute(x[:, :HALO], "lon", westward)
-    west = lax.ppermute(x[:, cols - HALO :], "lon", eastward)
+    east = lax.ppermute(sides[:, :HALO], "lon", westward)
+    west = lax.ppermute(sides[:, HALO:], "lon", eastward)
     return jnp.concatenate([east, west], axis=1)
 
 
@@ -300,15 +297,17 @@
     far_row = odd * (rows - HALO)
     near_row = (1 - odd) * (rows - HALO)
 
+    halo = pl.BlockSpec(memory_space=HALO_SPACE)
+    hbm = pl.BlockSpec(memory_space=pltpu.HBM)
     far_block = lax.dynamic_slice(x, (far_row, 0), (HALO, cols))
+    near_rows = lax.dynamic_slice(x, (near_row, 0), (HALO, cols))
+    held_x, far_block, near_rows = lax.optimization_barrier((x, far_block, near_rows))
+    lane = lax.broadcasted_iota(jnp.int32, (rows, LANES), 1)
+    sides = jnp.where(lane < HALO, held_x[:, :LANES], held_x[:, cols - LANES :])
+    lon = lon_halo(sides)
     far = lax.ppermute(far_block, "lat", pairs(1, count))
-    lon = lon_halo(x)
     near_block = jnp.concatenate(
-        [
-            lax.dynamic_slice(x, (near_row, 0), (HALO, cols)),
-            lax.dynamic_slice(lon, (near_row, 0), (HALO, LANES)),
-        ],
-        axis=1,
+        [near_rows, lax.dynamic_slice(lon, (near_row, 0), (HALO, LANES))], axis=1
     )
     near = lax.ppermute(near_block, "lat", pairs(0, count))
     corner_block = lax.dynamic_slice(lon, (far_row, 0), (HALO, LANES))
@@ -320,8 +319,6 @@
         jax.ShapeDtypeStruct((2, rows, cols), jnp.float32),
         jax.ShapeDtypeStruct((rows, cols), jnp.float32),
     ]
-    hbm = pl.BlockSpec(memory_space=pltpu.HBM)
-    halo = pl.BlockSpec(memory_space=HALO_SPACE)
     outs = pl.pallas_call(
         functools.partial(main_kernel, rows, tiles, total),
         out_shape=shapes,

time: 31.5 us -> 30.7 us (0.975)
  the two profiles are of different devices: /device:TPU:3 before, /device:TPU:9 now
where the time goes in v5:
time: 30.7 us; the launch traced here: 30.3 us
  Pallas kernels  15.3 us (50%)
  starting transfers between devices  8.45 us (28%)
  waiting for transfers between devices  3.93 us (13%)
  local copies, waits for them, and re-layouts  1.87 us (6%)
  between operations  0.71 us (2%)
    pallas_call x1, Pallas kernels, local(): pl.pallas_call(functools.partial(main_kernel, rows, tiles, total), out_sh...  10.4 us
    pallas_call x1, Pallas kernels, local(): pl.pallas_call(functools.partial(rim_kernel, rows, tiles, total, count),...  4.88 us
    ppermute x1, waiting for transfers between devices, lon_halo(): return lax.ppermute(sides, 'lon', [(0, 1), (1, 0)])  3.14 us
    ppermute x1, starting transfers between devices, local(): far = lax.ppermute(far_block, 'lat', pairs(1, count))  3.02 us
    ppermute x1, starting transfers between devices, local(): far_lon = lax.ppermute(corner_block, 'lat', pairs(1, count))  2.53 us
    ppermute x1, starting transfers between devices, local(): near = lax.ppermute(near_block, 'lat', pairs(0, count))  1.6 us
    dynamic_slice x1, local copies, waits for them, and re-layouts, local(): near_rows = lax.dynamic_slice(x, (near_row, 0), (HALO, cols))  1.44 us
    ppermute x1, starting transfers between devices, lon_halo(): return lax.ppermute(sides, 'lon', [(0, 1), (1, 0)])  1.3 us
  transfers between devices with their start and end apart: 4, of which 2 were waited for; matrix products, arithmetic and copies ran while one was open for 0% of the time, Pallas kernels for 34%

profile of v5, /device:TPU:9, one launch (start us, length us, event | category | flops | bytes accessed | tf_op | source)
XLA Modules:
  0.0 30.3 jit_solution(14630493170461029085)
XLA Ops:
  0.6 0.0 copy-start
  0.7 1.4 %constant_dynamic-slice_fusion.2 = (f32[64,2048]{1,0:T(8,128)S(1)}, f32[64,2048]{1,0:T(8,128)S(1)}) fusion(f32[256,2048]{1,0:T(8,128)} %x.3, s32[]{:T(128)S(6)} %select_n.13, s32[]{:T(128)S(6)} %select_n.12), kind=kLoop, calls=%fused_computation.4 | loop fusion | bytes 2097160 | tf_op jit(solution)/shard_map/dynamic_slice | solution.py:303
  2.1 0.4 %copy-done = f32[256,2048]{1,0:T(8,128)S(1)} copy-done((f32[256,2048]{1,0:T(8,128)S(1)}, f32[256,2048]{1,0:T(8,128)}, u32[]{:S(2)}) %copy-start) | copy-done | bytes 2097176
  2.6 1.3 %collective-permute-start = (f32[256,128]{1,0:T(8,128)S(1)}, f32[256,128]{1,0:T(8,128)S(1)}, u32[]{:S(2)}, u32[]{:S(2)}) collective-permute-start(f32[256,128]{1,0:T(8,128)S(1)} %slice_select_fusion), channel_id=1, source_target_pairs={{0,1},{1,0},{2,3},{3,2},{4,5},{5,4},{6,7},{7,6},{8,9},{9,8},{10,11... | collective-permute-start | bytes 393224 | tf_op jit(solution)/shard_map/ppermute | solution.py:278
  3.9 3.1 %collective-permute-done.lon = f32[256,128]{1,0:T(8,128)S(1)} collective-permute-done((f32[256,128]{1,0:T(8,128)S(1)}, f32[256,128]{1,0:T(8,128)S(1)}, u32[]{:S(2)}, u32[]{:S(2)}) %collective-permute-start) | collective-permute-done | bytes 131104 | tf_op jit(solution)/shard_map/ppermute | solution.py:278
  7.1 1.6 %collective-permute-start.3 = (f32[64,2176]{1,0:T(8,128)S(1)}, f32[64,2176]{1,0:T(8,128)S(1)}, u32[]{:S(2)}, u32[]{:S(2)}) collective-permute-start(f32[64,2176]{1,0:T(8,128)S(1)} %pad_maximum_fusion), channel_id=1, source_target_pairs={{0,2},{4,6},{8,10},{12,14},{16,18},{20,22},{24,26},{28,30},{2,0},{... | collective-permute-start | bytes 1671176 | tf_op jit(solution)/shard_map/ppermute | solution.py:312
  8.7 3.0 %collective-permute-start.1 = (f32[64,2048]{1,0:T(8,128)S(1)}, f32[64,2048]{1,0:T(8,128)S(1)}, u32[]{:S(2)}, u32[]{:S(2)}) collective-permute-start(f32[64,2048]{1,0:T(8,128)S(1)} %get-tuple-element.10), channel_id=1, source_target_pairs={{2,4},{6,8},{10,12},{14,16},{18,20},{22,24},{26,28},{4,2},{8,6},{1... | collective-permute-start | bytes 1572872 | tf_op jit(solution)/shard_map/ppermute | solution.py:308
  11.7 2.5 %collective-permute-start.2 = (f32[64,128]{1,0:T(8,128)S(1)}, f32[64,128]{1,0:T(8,128)S(1)}, u32[]{:S(2)}, u32[]{:S(2)}) collective-permute-start(f32[64,128]{1,0:T(8,128)S(1)} %get-tuple-element.18), channel_id=1, source_target_pairs={{2,4},{6,8},{10,12},{14,16},{18,20},{22,24},{26,28},{4,2},{8,6},{1... | collective-permute-start | bytes 98312 | tf_op jit(solution)/shard_map/ppermute | solution.py:314
  14.2 0.0 collective-permute-done.3.near
  14.2 10.4 %stencil_main.1 = (f32[256,2048]{1,0:T(8,128)}, f32[2,256,2048]{2,1,0:T(8,128)}, f32[256,2048]{1,0:T(8,128)}) custom-call(f32[256,2048]{1,0:T(8,128)S(1)} %copy-done, f32[256,128]{1,0:T(8,128)S(1)} %collective-permute-done.lon, f32[64,2176]{1,0:T(8,128)S(1)} %collective-permute-done.3.near), custom_call_target="tpu_custom_call" | custom-call | flops 78643200 | bytes 9437184 | tf_op jit(solution)/shard_map/stencil_main/pallas_call | solution.py:322
  24.7 0.8 %collective-permute-done.2.far_lon = f32[64,128]{1,0:T(8,128)S(1)} collective-permute-done((f32[64,128]{1,0:T(8,128)S(1)}, f32[64,128]{1,0:T(8,128)S(1)}, u32[]{:S(2)}, u32[]{:S(2)}) %collective-permute-start.2) | collective-permute-done | bytes 32800 | tf_op jit(solution)/shard_map/ppermute | solution.py:314
  25.5 0.0 collective-permute-done.1.far
  25.5 4.9 %stencil_rim.1 = (f32[256,2048]{1,0:T(8,128)}, f32[2,256,2048]{2,1,0:T(8,128)}, f32[256,2048]{1,0:T(8,128)}) custom-call(f32[256,2048]{1,0:T(8,128)S(1)} %copy-done, f32[256,128]{1,0:T(8,128)S(1)} %collective-permute-done.lon, f32[64,2048]{1,0:T(8,128)S(1)} %collective-permute-done.1.far, ...), custom_call_target="tpu_custom_call", output_to_operand_aliasing={{0}: (4, {}), {1}: (5, {}), {2}: (6, {})} | custom-call | flops 26214400 | bytes 3145728 | tf_op jit(solution)/shard_map/stencil_rim/pallas_call | solution.py:333
  (4 shorter events, 0.1 us)
Async XLA Ops:
  0.6 1.9 %copy-start = (f32[256,2048]{1,0:T(8,128)S(1)}, f32[256,2048]{1,0:T(8,128)}, u32[]{:S(2)}) copy-start(f32[256,2048]{1,0:T(8,128)} %x.3) | copy-start | bytes 6291460
  2.6 4.4 %collective-permute-start = (f32[256,128]{1,0:T(8,128)S(1)}, f32[256,128]{1,0:T(8,128)S(1)}, u32[]{:S(2)}, u32[]{:S(2)}) collective-permute-start(f32[256,128]{1,0:T(8,128)S(1)} %slice_select_fusion), channel_id=1, source_target_pairs={{0,1},{1,0},{2,3},{3,2},{4,5},{5,4},{6,7},{7,6},{8,9},{9,8},{10,11... | collective-permute-start | bytes 393224 | tf_op jit(solution)/shard_map/ppermute | solution.py:278
  7.1 7.2 %collective-permute-start.3 = (f32[64,2176]{1,0:T(8,128)S(1)}, f32[64,2176]{1,0:T(8,128)S(1)}, u32[]{:S(2)}, u32[]{:S(2)}) collective-permute-start(f32[64,2176]{1,0:T(8,128)S(1)} %pad_maximum_fusion), channel_id=1, source_target_pairs={{0,2},{4,6},{8,10},{12,14},{16,18},{20,22},{24,26},{28,30},{2,0},{... | collective-permute-start | bytes 1671176 | tf_op jit(solution)/shard_map/ppermute | solution.py:312
  8.7 16.8 %collective-permute-start.1 = (f32[64,2048]{1,0:T(8,128)S(1)}, f32[64,2048]{1,0:T(8,128)S(1)}, u32[]{:S(2)}, u32[]{:S(2)}) collective-permute-start(f32[64,2048]{1,0:T(8,128)S(1)} %get-tuple-element.10), channel_id=1, source_target_pairs={{2,4},{6,8},{10,12},{14,16},{18,20},{22,24},{26,28},{4,2},{8,6},{1... | collective-permute-start | bytes 1572872 | tf_op jit(solution)/shard_map/ppermute | solution.py:308
  11.7 13.8 %collective-permute-start.2 = (f32[64,128]{1,0:T(8,128)S(1)}, f32[64,128]{1,0:T(8,128)S(1)}, u32[]{:S(2)}, u32[]{:S(2)}) collective-permute-start(f32[64,128]{1,0:T(8,128)S(1)} %get-tuple-element.18), channel_id=1, source_target_pairs={{2,4},{6,8},{10,12},{14,16},{18,20},{22,24},{26,28},{4,2},{8,6},{1... | collective-permute-start | bytes 98312 | tf_op jit(solution)/shard_map/ppermute | solution.py:314

commit v6 on v5

--- a/solution.py
+++ b/solution.py
@@ -109,7 +109,10 @@
                     q[k][0, j, pl.ds(row, SUB), :] = low
                     q[k][1, j, pl.ds(row, SUB), :] = high
                 if old:
-                    tile_cache[j, k] = (low, high, before, after)
+                    down, up = after - low, high - before
+                    if j in tile_cache:
+                        down, up = tile_cache[j][0] + down, tile_cache[j][1] + up
+                    tile_cache[j] = (down, up)
 
     def warm(step, active):
         new_boxes(step * SUB, active, {})
@@ -127,12 +130,7 @@
         cache = {"old": True}
         new_boxes(base, range(SCALES), cache)
         for j in range(tiles):
-            falling = rising = None
-            for k in range(SCALES):
-                low, high, old_low, old_high = cache[j, k]
-                down, up = old_high - low, high - old_low
-                falling = down if falling is None else falling + down
-                rising = up if rising is None else rising + up
+            falling, rising = cache[j]
             held[0, j] = falling + rising
             held[1, j] = falling - rising
 
@@ -146,7 +144,7 @@
 
     count = row_count // SUB
 
-    @pl.loop(0, count, unroll=4)
+    @pl.loop(0, count, unroll=8)
     def _(step):
         finish(jnp.maximum(step - 1, 0))
         sums(step)

time: 30.7 us -> 30.5 us (level)
  no operation moved by 1% of the time
where the time goes in v6:
time: 30.5 us; the launch traced here: 30.4 us
  Pallas kernels  15.1 us (50%)
  starting transfers between devices  8.45 us (28%)
  waiting for transfers between devices  4.15 us (14%)
  local copies, waits for them, and re-layouts  1.87 us (6%)
  between operations  0.71 us (2%)
    pallas_call x1, Pallas kernels, local(): pl.pallas_call(functools.partial(main_kernel, rows, tiles, total), out_sh...  10.2 us
    pallas_call x1, Pallas kernels, local(): pl.pallas_call(functools.partial(rim_kernel, rows, tiles, total, count),...  4.89 us
    ppermute x1, waiting for transfers between devices, lon_halo(): return lax.ppermute(sides, 'lon', [(0, 1), (1, 0)])  3.14 us
    ppermute x1, starting transfers between devices, local(): far = lax.ppermute(far_block, 'lat', pairs(1, count))  3.02 us
    ppermute x1, starting transfers between devices, local(): far_lon = lax.ppermute(corner_block, 'lat', pairs(1, count))  2.53 us
    ppermute x1, starting transfers between devices, local(): near = lax.ppermute(near_block, 'lat', pairs(0, count))  1.6 us
    dynamic_slice x1, local copies, waits for them, and re-layouts, local(): near_rows = lax.dynamic_slice(x, (near_row, 0), (HALO, cols))  1.44 us
    ppermute x1, starting transfers between devices, lon_halo(): return lax.ppermute(sides, 'lon', [(0, 1), (1, 0)])  1.3 us
  transfers between devices with their start and end apart: 4, of which 2 were waited for; matrix products, arithmetic and copies ran while one was open for 0% of the time, Pallas kernels for 34%

profile of v6, /device:TPU:9, one launch (start us, length us, event | category | flops | bytes accessed | tf_op | source)
XLA Modules:
  0.0 30.4 jit_solution(3445945470144745035)
XLA Ops:
  0.6 0.0 copy-start
  0.7 1.4 %constant_dynamic-slice_fusion.2 = (f32[64,2048]{1,0:T(8,128)S(1)}, f32[64,2048]{1,0:T(8,128)S(1)}) fusion(f32[256,2048]{1,0:T(8,128)} %x.3, s32[]{:T(128)S(6)} %select_n.13, s32[]{:T(128)S(6)} %select_n.12), kind=kLoop, calls=%fused_computation.4 | loop fusion | bytes 2097160 | tf_op jit(solution)/shard_map/dynamic_slice | solution.py:301
  2.1 0.4 %copy-done = f32[256,2048]{1,0:T(8,128)S(1)} copy-done((f32[256,2048]{1,0:T(8,128)S(1)}, f32[256,2048]{1,0:T(8,128)}, u32[]{:S(2)}) %copy-start) | copy-done | bytes 2097176
  2.6 1.3 %collective-permute-start = (f32[256,128]{1,0:T(8,128)S(1)}, f32[256,128]{1,0:T(8,128)S(1)}, u32[]{:S(2)}, u32[]{:S(2)}) collective-permute-start(f32[256,128]{1,0:T(8,128)S(1)} %slice_select_fusion), channel_id=1, source_target_pairs={{0,1},{1,0},{2,3},{3,2},{4,5},{5,4},{6,7},{7,6},{8,9},{9,8},{10,11... | collective-permute-start | bytes 393224 | tf_op jit(solution)/shard_map/ppermute | solution.py:276
  3.9 3.1 %collective-permute-done.lon = f32[256,128]{1,0:T(8,128)S(1)} collective-permute-done((f32[256,128]{1,0:T(8,128)S(1)}, f32[256,128]{1,0:T(8,128)S(1)}, u32[]{:S(2)}, u32[]{:S(2)}) %collective-permute-start) | collective-permute-done | bytes 131104 | tf_op jit(solution)/shard_map/ppermute | solution.py:276
  7.1 1.6 %collective-permute-start.3 = (f32[64,2176]{1,0:T(8,128)S(1)}, f32[64,2176]{1,0:T(8,128)S(1)}, u32[]{:S(2)}, u32[]{:S(2)}) collective-permute-start(f32[64,2176]{1,0:T(8,128)S(1)} %pad_maximum_fusion), channel_id=1, source_target_pairs={{0,2},{4,6},{8,10},{12,14},{16,18},{20,22},{24,26},{28,30},{2,0},{... | collective-permute-start | bytes 1671176 | tf_op jit(solution)/shard_map/ppermute | solution.py:310
  8.7 3.0 %collective-permute-start.1 = (f32[64,2048]{1,0:T(8,128)S(1)}, f32[64,2048]{1,0:T(8,128)S(1)}, u32[]{:S(2)}, u32[]{:S(2)}) collective-permute-start(f32[64,2048]{1,0:T(8,128)S(1)} %get-tuple-element.10), channel_id=1, source_target_pairs={{2,4},{6,8},{10,12},{14,16},{18,20},{22,24},{26,28},{4,2},{8,6},{1... | collective-permute-start | bytes 1572872 | tf_op jit(solution)/shard_map/ppermute | solution.py:306
  11.7 2.5 %collective-permute-start.2 = (f32[64,128]{1,0:T(8,128)S(1)}, f32[64,128]{1,0:T(8,128)S(1)}, u32[]{:S(2)}, u32[]{:S(2)}) collective-permute-start(f32[64,128]{1,0:T(8,128)S(1)} %get-tuple-element.18), channel_id=1, source_target_pairs={{2,4},{6,8},{10,12},{14,16},{18,20},{22,24},{26,28},{4,2},{8,6},{1... | collective-permute-start | bytes 98312 | tf_op jit(solution)/shard_map/ppermute | solution.py:312
  14.2 0.0 collective-permute-done.3.near
  14.2 10.2 %stencil_main.1 = (f32[256,2048]{1,0:T(8,128)}, f32[2,256,2048]{2,1,0:T(8,128)}, f32[256,2048]{1,0:T(8,128)}) custom-call(f32[256,2048]{1,0:T(8,128)S(1)} %copy-done, f32[256,128]{1,0:T(8,128)S(1)} %collective-permute-done.lon, f32[64,2176]{1,0:T(8,128)S(1)} %collective-permute-done.3.near), custom_call_target="tpu_custom_call" | custom-call | flops 78643200 | bytes 9437184 | tf_op jit(solution)/shard_map/stencil_main/pallas_call | solution.py:320
  24.5 1.0 %collective-permute-done.2.far_lon = f32[64,128]{1,0:T(8,128)S(1)} collective-permute-done((f32[64,128]{1,0:T(8,128)S(1)}, f32[64,128]{1,0:T(8,128)S(1)}, u32[]{:S(2)}, u32[]{:S(2)}) %collective-permute-start.2) | collective-permute-done | bytes 32800 | tf_op jit(solution)/shard_map/ppermute | solution.py:312
  25.5 0.0 collective-permute-done.1.far
  25.5 4.9 %stencil_rim.1 = (f32[256,2048]{1,0:T(8,128)}, f32[2,256,2048]{2,1,0:T(8,128)}, f32[256,2048]{1,0:T(8,128)}) custom-call(f32[256,2048]{1,0:T(8,128)S(1)} %copy-done, f32[256,128]{1,0:T(8,128)S(1)} %collective-permute-done.lon, f32[64,2048]{1,0:T(8,128)S(1)} %collective-permute-done.1.far, ...), custom_call_target="tpu_custom_call", output_to_operand_aliasing={{0}: (4, {}), {1}: (5, {}), {2}: (6, {})} | custom-call | flops 26214400 | bytes 3145728 | tf_op jit(solution)/shard_map/stencil_rim/pallas_call | solution.py:331
  (4 shorter events, 0.1 us)
Async XLA Ops:
  0.6 1.9 %copy-start = (f32[256,2048]{1,0:T(8,128)S(1)}, f32[256,2048]{1,0:T(8,128)}, u32[]{:S(2)}) copy-start(f32[256,2048]{1,0:T(8,128)} %x.3) | copy-start | bytes 6291460
  2.6 4.4 %collective-permute-start = (f32[256,128]{1,0:T(8,128)S(1)}, f32[256,128]{1,0:T(8,128)S(1)}, u32[]{:S(2)}, u32[]{:S(2)}) collective-permute-start(f32[256,128]{1,0:T(8,128)S(1)} %slice_select_fusion), channel_id=1, source_target_pairs={{0,1},{1,0},{2,3},{3,2},{4,5},{5,4},{6,7},{7,6},{8,9},{9,8},{10,11... | collective-permute-start | bytes 393224 | tf_op jit(solution)/shard_map/ppermute | solution.py:276
  7.1 7.2 %collective-permute-start.3 = (f32[64,2176]{1,0:T(8,128)S(1)}, f32[64,2176]{1,0:T(8,128)S(1)}, u32[]{:S(2)}, u32[]{:S(2)}) collective-permute-start(f32[64,2176]{1,0:T(8,128)S(1)} %pad_maximum_fusion), channel_id=1, source_target_pairs={{0,2},{4,6},{8,10},{12,14},{16,18},{20,22},{24,26},{28,30},{2,0},{... | collective-permute-start | bytes 1671176 | tf_op jit(solution)/shard_map/ppermute | solution.py:310
  8.7 16.8 %collective-permute-start.1 = (f32[64,2048]{1,0:T(8,128)S(1)}, f32[64,2048]{1,0:T(8,128)S(1)}, u32[]{:S(2)}, u32[]{:S(2)}) collective-permute-start(f32[64,2048]{1,0:T(8,128)S(1)} %get-tuple-element.10), channel_id=1, source_target_pairs={{2,4},{6,8},{10,12},{14,16},{18,20},{22,24},{26,28},{4,2},{8,6},{1... | collective-permute-start | bytes 1572872 | tf_op jit(solution)/shard_map/ppermute | solution.py:306
  11.7 13.8 %collective-permute-start.2 = (f32[64,128]{1,0:T(8,128)S(1)}, f32[64,128]{1,0:T(8,128)S(1)}, u32[]{:S(2)}, u32[]{:S(2)}) collective-permute-start(f32[64,128]{1,0:T(8,128)S(1)} %get-tuple-element.18), channel_id=1, source_target_pairs={{2,4},{6,8},{10,12},{14,16},{18,20},{22,24},{26,28},{4,2},{8,6},{1... | collective-permute-start | bytes 98312 | tf_op jit(solution)/shard_map/ppermute | solution.py:312
